TPU v7x, 16 devices: a 4x2x1 block of a 4x4x8 slice. The times are simulated.
16 devices in a mesh: dp: 2 (over y, z), ep: 8 (over x, core).
Axes of the slice: x: 4, y: 2, z: 1, core: 2. Of those that a mesh axis runs over, the one named last changes fastest.
The devices are a block of a 4x4x8 slice.
Arguments:
- hidden_in: bfloat16 [768, 1536], P(('dp', 'ep')), parts along dimension 0
- norm_gain: float32 [1536], replicated
- router_w: float32 [64, 1536], replicated
- w_gate: bfloat16 [64, 1536, 512], P('ep')
- w_up: bfloat16 [64, 1536, 512], P('ep')
- w_down: bfloat16 [64, 512, 1536], P('ep')
- ws_gate: bfloat16 [1536, 1024], replicated
- ws_up: bfloat16 [1536, 1024], replicated
- ws_down: bfloat16 [1024, 1536], replicated
- expert_ids: int32 [768, 6], P(('dp', 'ep')), parts along dimension 0
Outputs:
- output: bfloat16 [768, 1536], P(('dp', 'ep')), parts along dimension 0
There are 2 independent parts. A program takes and returns all parts, laid end to end along the dimension named above; an argument that names none is the same for every part.
All inputs are finite; a program needn't handle non-finite values.
Results may differ from a plain program's by a relative error of at most 0.00425754.
Values are sent between devices in bfloat16 or wider.
A program may use at most 768 MiB of HBM per device.

v0:
```python
import jax
import jax.numpy as jnp
from jax import lax
from jax.sharding import PartitionSpec as P

NORM_EPS = 1e-6
ROUTE_SCALE = 2.5
GROUPS = 8
GROUP_LIMIT = 4


def rms_norm(x_rows, norm_gain):
    x_f32 = x_rows.astype(jnp.float32)
    inv_rms = lax.rsqrt(jnp.mean(x_f32 * x_f32, axis=-1, keepdims=True) + NORM_EPS)
    return (x_f32 * inv_rms * norm_gain).astype(jnp.bfloat16)


def route_gates(x_norm, router_w, expert_ids):
    logits = jnp.einsum("td,nd->tn", x_norm.astype(jnp.float32), router_w, precision=lax.Precision.HIGHEST, preferred_element_type=jnp.float32)
    picked = jnp.take_along_axis(jax.nn.sigmoid(logits), expert_ids, axis=1)
    return ROUTE_SCALE * picked / jnp.sum(picked, axis=1, keepdims=True)


def swiglu(tok_rows, gate_mat, up_mat, down_mat):
    h_gate = jnp.dot(tok_rows, gate_mat, preferred_element_type=jnp.float32)
    h_up = jnp.dot(tok_rows, up_mat, preferred_element_type=jnp.float32)
    hidden = (jax.nn.silu(h_gate) * h_up).astype(jnp.bfloat16)
    return jnp.dot(hidden, down_mat, preferred_element_type=jnp.float32).astype(jnp.bfloat16)


def expert_stack(expert_in, w_gate, w_up, w_down):
    h_gate = jnp.einsum("ecd,edi->eci", expert_in, w_gate, preferred_element_type=jnp.float32)
    h_up = jnp.einsum("ecd,edi->eci", expert_in, w_up, preferred_element_type=jnp.float32)
    hidden = (jax.nn.silu(h_gate) * h_up).astype(jnp.bfloat16)
    return jnp.einsum("eci,eid->ecd", hidden, w_down, preferred_element_type=jnp.float32).astype(jnp.bfloat16)


def solution(mesh):
    ep_size = mesh.shape["ep"]

    def local_block(hidden_in, norm_gain, router_w, w_gate, w_up, w_down, ws_gate, ws_up, ws_down, expert_ids):
        tok_dev, top_k = expert_ids.shape
        model_dim = hidden_in.shape[1]
        exp_dev = w_gate.shape[0]
        pair_cap = GROUPS * ((top_k + GROUP_LIMIT - 1) // GROUP_LIMIT) * tok_dev // ep_size
        recv_cap = pair_cap * ep_size
        exp_cap = recv_cap // exp_dev
        x_norm = rms_norm(hidden_in, norm_gain)
        gate_vals = route_gates(x_norm, router_w, expert_ids)
        shared_out = swiglu(x_norm, ws_gate, ws_up, ws_down)

        flat_ids = expert_ids.reshape(-1)
        dest_dev = flat_ids // exp_dev
        dest_hot = (dest_dev[:, None] == jnp.arange(ep_size, dtype=jnp.int32)[None, :]).astype(jnp.int32)
        dest_rank = jnp.sum((jnp.cumsum(dest_hot, axis=0) - 1) * dest_hot, axis=1)
        send_slot = dest_dev * pair_cap + dest_rank
        pair_tok = jnp.arange(tok_dev * top_k, dtype=jnp.int32) // top_k
        slot_tok = jnp.full((recv_cap,), tok_dev, jnp.int32).at[send_slot].set(pair_tok)
        slot_exp = jnp.full((recv_cap,), -1, jnp.int32).at[send_slot].set(flat_ids % exp_dev)
        send_rows = jnp.take(x_norm, slot_tok, axis=0, mode="fill", fill_value=0)
        recv_rows = lax.all_to_all(send_rows, "ep", 0, 0, tiled=True)
        recv_exp = lax.all_to_all(slot_exp, "ep", 0, 0, tiled=True)

        exp_hot = (recv_exp[:, None] == jnp.arange(exp_dev, dtype=jnp.int32)[None, :]).astype(jnp.int32)
        exp_rank = jnp.sum((jnp.cumsum(exp_hot, axis=0) - 1) * exp_hot, axis=1)
        buf_slot = jnp.where(recv_exp >= 0, recv_exp * exp_cap + exp_rank, recv_cap)
        buf_row = jnp.full((recv_cap,), recv_cap, jnp.int32).at[buf_slot].set(jnp.arange(recv_cap, dtype=jnp.int32), mode="drop")
        expert_in = jnp.take(recv_rows, buf_row, axis=0, mode="fill", fill_value=0).reshape(exp_dev, exp_cap, model_dim)
        expert_out = expert_stack(expert_in, w_gate, w_up, w_down).reshape(recv_cap, model_dim)
        back_rows = jnp.take(expert_out, buf_slot, axis=0, mode="fill", fill_value=0)
        returned = lax.all_to_all(back_rows, "ep", 0, 0, tiled=True)

        pair_out = jnp.take(returned, send_slot, axis=0).reshape(tok_dev, top_k, model_dim)
        routed = jnp.sum(gate_vals[:, :, None] * pair_out.astype(jnp.float32), axis=1)
        return (hidden_in.astype(jnp.float32) + shared_out.astype(jnp.float32) + routed).astype(jnp.bfloat16)

    row_spec = P(("dp", "ep"), None)
    in_specs = (row_spec, P(), P(), P("ep"), P("ep"), P("ep"), P(), P(), P(), row_spec)
    return jax.shard_map(local_block, mesh=mesh, in_specs=in_specs, out_specs=row_spec, check_vma=False)
```

profile of v0, /device:TPU:112, one launch (start us, length us, event | category | flops | bytes accessed | tf_op | source)
XLA Modules:
  0.0 153.3 jit_solution(12474387893007818118)
XLA Ops:
  2.5 2.9 %scatter_custom_fusion.1 = s32[768]{0:T(1024)S(1)} fusion(s32[288]{0:T(512)S(1)} %fusion.37, s32[288]{0:T(512)S(1)} %get-tuple-element.10, s32[]{:T(128)} %constant.118.clone.1), kind=kCustom, calls=%fused_computation.95 | custom fusion | bytes 3076 | tf_op jit(solution)/shard_map/scatter | solution.py:59
  6.1 5.3 %all-to-all-start.1 = ((s32[8,96,1]{1,2,0:T(1,128)}), s32[8,96,1]{1,2,0:T(1,128)S(1)}, u32[]{:S(2)}, u32[]{:S(2)}) async-start(s32[8,96,1]{1,2,0:T(1,128)} %all_to_all.22), calls=%async_computation.1 | async-start | bytes 8192 | tf_op jit(solution)/shard_map/all_to_all | solution.py:62
  11.4 2.9 %scatter_custom_fusion = s32[768]{0:T(1024)S(1)} fusion(s32[288]{0:T(512)S(1)} %fusion.37, s32[288]{0:T(512)S(1)} %add_select_fusion.3, s32[]{:T(128)} %constant.123.clone.1), kind=kCustom, calls=%fused_computation.99 | custom fusion | bytes 3076 | tf_op jit(solution)/shard_map/scatter | solution.py:58
  16.5 3.8 %gather_fusion = bf16[768,1536]{1,0:T(8,128)(2,1)} fusion(bf16[48,1536]{1,0:T(8,128)(2,1)S(1)} %fusion.11, s32[1024]{0:T(1024)S(1)} %pad_clamp_fusion.3), kind=kCustom, calls=%fused_computation.2 | custom fusion | bytes 4721664 | tf_op jit(solution)/shard_map/jit(_take)/gather | solution.py:60
  20.4 3.3 %broadcast_select_fusion.2 = bf16[8,96,1536]{2,1,0:T(8,128)(2,1)} fusion(bf16[8,96,1536]{2,1,0:T(8,128)(2,1)} %bitcast.40, pred[8,96]{1,0:T(8,128)(4,1)S(1)} %broadcast_in_dim.59), kind=kLoop, calls=%fused_computation.12 | loop fusion | flops 1179648 | bytes 4719360 | tf_op jit(solution)/shard_map/jit(_take)/select_n | solution.py:60
  23.6 4.8 %all-to-all-start = ((bf16[8,96,1536]{2,1,0:T(8,128)(2,1)}), bf16[8,96,1536]{2,1,0:T(8,128)(2,1)}, u32[]{:S(2)}, u32[]{:S(2)}) async-start(bf16[8,96,1536]{2,1,0:T(8,128)(2,1)} %broadcast_select_fusion.2), calls=%async_computation | async-start | bytes 4718592 | tf_op jit(solution)/shard_map/all_to_all | solution.py:61
  29.8 1.7 %reduce-window.16 = s32[8,6,128]{2,0,1:T(8,128)S(1)} reduce-window(s32[8,6,128]{2,0,1:T(8,128)S(1)} %fusion.19, s32[]{:T(128)} %constant.110.clone.1), window={size=1x1x128 pad=0_0x0_0x127_0}, to_apply=%region_7.8 | reduce-window | flops 780288 | bytes 49156 | tf_op jit(solution)/shard_map/reduce-window.2
  32.3 3.6 %scatter_custom_fusion.2 = s32[768]{0:T(1024)S(1)} fusion(s32[768]{0:T(1024)S(1)} %fusion.26, s32[768]{0:T(1024)S(1)} %iota.18, s32[]{:T(128)} %constant.121.clone.1), kind=kCustom, calls=%fused_computation.97 | custom fusion | bytes 3076 | tf_op jit(solution)/shard_map/scatter | solution.py:67
  35.9 22.5 %all-to-all-done = bf16[8,96,1536]{2,1,0:T(8,128)(2,1)} async-done(((bf16[8,96,1536]{2,1,0:T(8,128)(2,1)}), bf16[8,96,1536]{2,1,0:T(8,128)(2,1)}, u32[]{:S(2)}, u32[]{:S(2)}) %all-to-all-start) | async-done | bytes 2359328 | tf_op jit(solution)/shard_map/all_to_all | solution.py:61
  58.5 7.9 %gather_fusion.3 = bf16[768,1536]{1,0:T(8,128)(2,1)} fusion(bf16[768,1536]{1,0:T(8,128)(2,1)} %bitcast.8, s32[1024]{0:T(1024)S(1)} %pad_clamp_fusion.2), kind=kCustom, calls=%fused_computation.clone | custom fusion | bytes 4721664 | tf_op jit(solution)/shard_map/jit(_take)/gather | solution.py:68
  66.3 1.9 %broadcast_select_fusion.1 = bf16[768,1536]{1,0:T(8,128)(2,1)S(1)} fusion(bf16[768,1536]{1,0:T(8,128)(2,1)} %gather_fusion.3, pred[768]{0:T(1024)(128)(4,1)S(1)} %compare_and_fusion.1), kind=kLoop, calls=%fused_computation.11 | loop fusion | flops 1179648 | bytes 4719360 | tf_op jit(solution)/shard_map/jit(_take)/select_n | solution.py:68
  68.2 1.4 copy-done.1
  69.6 7.8 %fusion.47 = f32[8,96,512]{2,1,0:T(8,128)} fusion(bf16[8,96,1536]{2,1,0:T(8,128)(2,1)S(1)} %bitcast.37, bf16[8,1536,512]{2,1,0:T(8,128)(2,1)} %param.15), kind=kOutput, calls=%fused_computation.112 | convolution fusion | flops 1207959552 | bytes 16515072 | tf_op jit(solution)/shard_map/ecd,edi->eci/dot_general | solution.py:32
  77.4 14.9 %convolution_convert_fusion = bf16[8,96,1536]{2,1,0:T(8,128)(2,1)} fusion(bf16[8,512,1536]{2,1,0:T(8,128)(2,1)} %param.17, f32[8,96,512]{2,1,0:T(8,128)} %fusion.47, bf16[8,96,1536]{2,1,0:T(8,128)(2,1)} %bitcast.38, bf16[8,1536,512]{2,1,0:T(8,128)(2,1)} %param.16), kind=kOutput, calls=%fused_computation.8 | convolution fusion | flops 2419458048 | bytes 31457280 | tf_op jit(solution)/shard_map/eci,eid->ecd/dot_general | solution.py:35
  92.4 7.9 %gather_fusion.4 = bf16[768,1536]{1,0:T(8,128)(2,1)} fusion(bf16[768,1536]{1,0:T(8,128)(2,1)} %bitcast.36, s32[1024]{0:T(1024)S(1)} %pad_clamp_fusion.1), kind=kCustom, calls=%fused_computation.1.clone | custom fusion | bytes 4721664 | tf_op jit(solution)/shard_map/jit(_take)/gather | solution.py:70
  100.2 3.3 %broadcast_select_fusion = bf16[768,1536]{1,0:T(8,128)(2,1)} fusion(bf16[768,1536]{1,0:T(8,128)(2,1)} %gather_fusion.4, pred[768]{0:T(1024)(128)(4,1)S(1)} %get-tuple-element.8), kind=kLoop, calls=%fused_computation.10 | loop fusion | flops 1179648 | bytes 4719360 | tf_op jit(solution)/shard_map/jit(_take)/select_n | solution.py:70
  103.5 4.9 %all-to-all-start.2 = ((bf16[8,96,1536]{2,1,0:T(8,128)(2,1)}), bf16[8,96,1536]{2,1,0:T(8,128)(2,1)}, u32[]{:S(2)}, u32[]{:S(2)}) async-start(bf16[8,96,1536]{2,1,0:T(8,128)(2,1)} %bitcast.39), calls=%async_computation.2 | async-start | bytes 4718592 | tf_op jit(solution)/shard_map/all_to_all | solution.py:71
  110.4 2.5 %gather_fusion.2 = f32[288]{0:T(512)S(1)} fusion(f32[48,64]{1,0:T(8,128)S(1)} %fusion.7, s32[288]{0:T(512)S(1)} %reshape.289), kind=kCustom, calls=%fused_computation.4 | custom fusion | bytes 4608 | tf_op jit(solution)/shard_map/jit(take_along_axis)/gather | solution.py:20
  113.2 2.6 %fusion.44 = f32[48,1024]{1,0:T(8,128)S(1)} fusion(bf16[1536,1024]{1,0:T(8,128)(2,1)} %param.18, bf16[48,1536]{1,0:T(8,128)(2,1)S(1)} %copy-done.2, f32[1536]{0:T(1024)S(1)} %copy-done.3, f32[48]{0:T(128)S(1)} %add_rsqrt_fusion), kind=kOutput, calls=%fused_computation.110 | convolution fusion | flops 151289856 | bytes 3496128 | tf_op jit(solution)/shard_map/dot_general | solution.py:25
  115.8 22.1 %all-to-all-done.2 = bf16[8,96,1536]{2,1,0:T(8,128)(2,1)} async-done(((bf16[8,96,1536]{2,1,0:T(8,128)(2,1)}), bf16[8,96,1536]{2,1,0:T(8,128)(2,1)}, u32[]{:S(2)}, u32[]{:S(2)}) %all-to-all-start.2) | async-done | bytes 2359328 | tf_op jit(solution)/shard_map/all_to_all | solution.py:71
  138.0 6.1 %gather_fusion.1 = bf16[288,1536]{1,0:T(8,128)(2,1)} fusion(bf16[768,1536]{1,0:T(8,128)(2,1)} %bitcast.12, s32[1024]{0:T(1024)S(1)} %pad_clamp_fusion), kind=kCustom, calls=%fused_computation.3 | custom fusion | bytes 1770624 | tf_op jit(solution)/shard_map/jit(_take)/gather | solution.py:73
  144.1 2.2 %gather.23 = bf16[48,6,1536]{2,1,0:T(8,128)(2,1)} reshape(bf16[288,1536]{1,0:T(8,128)(2,1)} %gather_fusion.1) | data formatting | bytes 1769472 | tf_op jit(solution)/shard_map/jit(_take)/gather | solution.py:73
  146.3 3.2 %multiply_reduce_fusion = f32[48,1536]{1,0:T(8,128)} fusion(bf16[48,6,1536]{2,1,0:T(8,128)(2,1)} %gather.23, f32[48,6]{1,0:T(8,128)S(1)} %copy.50, pred[48,6]{1,0:T(8,128)(4,1)S(1)} %copy.53), kind=kLoop, calls=%fused_computation.9 | loop fusion | flops 1695744 | bytes 1181088 | tf_op jit(solution)/shard_map/reduce_sum | solution.py:74
  149.5 3.8 %fusion.3 = bf16[48,1536]{1,0:T(8,128)(2,1)} fusion(f32[48,1536]{1,0:T(8,128)} %multiply_reduce_fusion, bf16[1024,1536]{1,0:T(8,128)(2,1)S(1)} %copy-done, bf16[1536,1024]{1,0:T(8,128)(2,1)} %param.19, bf16[48,1536]{1,0:T(8,128)(2,1)S(1)} %copy-done.2, f32[48,1024]{1,0:T(8,128)S(1)} %fusion.44, f32[1536]{0:T(1024)S(1)} %copy-done.3, f32[48]{0:T(128)S(1)} %add_rsqrt_fusion), kind=kOutput, calls=%fused_computation.17 | convolution fusion | flops 303022080 | bytes 7084224 | tf_op jit(solution)/shard_map/dot_general | solution.py:28
  (65 shorter events, 9.7 us)
Async XLA Ops:
  0.0 149.5 %copy-start = (bf16[1024,1536]{1,0:T(8,128)(2,1)S(1)}, bf16[1024,1536]{1,0:T(8,128)(2,1)}, u32[]{:S(2)}) copy-start(bf16[1024,1536]{1,0:T(8,128)(2,1)} %param.20) | copy-start | bytes 9437188
  6.1 17.6 %all-to-all-start.1 = ((s32[8,96,1]{1,2,0:T(1,128)}), s32[8,96,1]{1,2,0:T(1,128)S(1)}, u32[]{:S(2)}, u32[]{:S(2)}) async-start(s32[8,96,1]{1,2,0:T(1,128)} %all_to_all.22), calls=%async_computation.1 | async-start | bytes 8192 | tf_op jit(solution)/shard_map/all_to_all | solution.py:62
  23.6 34.8 %all-to-all-start = ((bf16[8,96,1536]{2,1,0:T(8,128)(2,1)}), bf16[8,96,1536]{2,1,0:T(8,128)(2,1)}, u32[]{:S(2)}, u32[]{:S(2)}) async-start(bf16[8,96,1536]{2,1,0:T(8,128)(2,1)} %broadcast_select_fusion.2), calls=%async_computation | async-start | bytes 4718592 | tf_op jit(solution)/shard_map/all_to_all | solution.py:61
  68.2 1.4 copy-start.1
  103.5 5.1 %copy-start.4 = (s32[48,6]{0,1:T(8,128)S(1)}, s32[48,6]{0,1:T(8,128)}, u32[]{:S(2)}) copy-start(s32[48,6]{0,1:T(8,128)} %param.21) | copy-start | bytes 3460
  103.5 5.5 %copy-start.2 = (bf16[48,1536]{1,0:T(8,128)(2,1)S(1)}, bf16[48,1536]{1,0:T(8,128)(2,1)}, u32[]{:S(2)}) copy-start(bf16[48,1536]{1,0:T(8,128)(2,1)} %param.12) | copy-start | bytes 442372
  103.5 5.5 %copy-start.3 = (f32[1536]{0:T(1024)S(1)}, f32[1536]{0:T(1024)}, u32[]{:S(2)}) copy-start(f32[1536]{0:T(1024)} %param.13) | copy-start | bytes 18436
  103.5 34.5 %all-to-all-start.2 = ((bf16[8,96,1536]{2,1,0:T(8,128)(2,1)}), bf16[8,96,1536]{2,1,0:T(8,128)(2,1)}, u32[]{:S(2)}, u32[]{:S(2)}) async-start(bf16[8,96,1536]{2,1,0:T(8,128)(2,1)} %bitcast.39), calls=%async_computation.2 | async-start | bytes 4718592 | tf_op jit(solution)/shard_map/all_to_all | solution.py:71
where the time goes:
time: 154 us; the launch traced here: 153 us
  local copies, waits for them, and re-layouts  45.2 us (29%)
  waiting for transfers between devices  44.6 us (29%)
  matrix products  30.6 us (20%)
  other arithmetic  17.6 us (11%)
  starting transfers between devices  15 us (10%)
    all_to_all x1, waiting for transfers between devices, local_block(): recv_rows = lax.all_to_all(send_rows, 'ep', 0, 0, tiled=True)  22.5 us
    all_to_all x1, waiting for transfers between devices, local_block(): returned = lax.all_to_all(back_rows, 'ep', 0, 0, tiled=True)  22.1 us
    dot_general x1, matrix products, expert_stack(): jnp.einsum('eci,eid->ecd', hidden, w_down, preferred_element_type=jnp.flo...  14.9 us
    gather x2, local copies, waits for them, and re-layouts, local_block(): jnp.take(returned, send_slot, axis=0).reshape(tok_dev, top_k, model_dim)  8.34 us
    gather x1, local copies, waits for them, and re-layouts, local_block(): jnp.take(recv_rows, buf_row, axis=0, mode='fill', fill_value=0)  7.86 us
    gather x1, local copies, waits for them, and re-layouts, local_block(): jnp.take(expert_out, buf_slot, axis=0, mode='fill', fill_value=0)  7.86 us
    dot_general x1, matrix products, expert_stack(): jnp.einsum('ecd,edi->eci', expert_in, w_gate, preferred_element_type=jnp....  7.84 us
    all_to_all x1, starting transfers between devices, local_block(): recv_exp = lax.all_to_all(slot_exp, 'ep', 0, 0, tiled=True)  5.3 us
  transfers between devices with their start and end apart: 3, of which 2 were waited for; matrix products, arithmetic and copies ran while one was open for 18% of the time, Pallas kernels for 0%

commit v1 on v0

v1 whole, which is shorter than its diff:
```python
import functools

import jax
import jax.numpy as jnp
from jax import lax
from jax.experimental import pallas as pl
from jax.experimental.pallas import tpu as pltpu
from jax.sharding import PartitionSpec as P

NORM_EPS = 1e-6
ROUTE_SCALE = 2.5
GROUPS = 8
GROUP_LIMIT = 4
CORES = 2
COLS = 256
MESH = pl.DeviceIdType.MESH
F32 = jnp.float32
BF16 = jnp.bfloat16


def dot(a, b):
    return jnp.dot(a, b, preferred_element_type=F32)


def dot_t(a, b):
    return lax.dot_general(a, b, (((1,), (1,)), ((), ())), preferred_element_type=F32)


def split3(v):
    hi = v.astype(BF16)
    rest = v - hi.astype(F32)
    mid = rest.astype(BF16)
    low = (rest - mid.astype(F32)).astype(BF16)
    return hi, mid, low


def moe_kernel(ep_size, cap, hid_h, gain_h, rw_h, wg_h, wu_h, wd_h, sg_h, su_h, sd_h, ids_h, out_ref,
               hid, gain, rw, ids, wg, wu, wd, sg, su, sd, x_all, gt_send, gt_all, p_all, ga, a_hi, a_mid, a_low,
               xg, hbuf, ybuf, sbuf, d2d, tbuf, hopa, hopb, rela, relb, froml, fromr, hsh, shared,
               in_sem, w_sem, send_sem, recv_sem):
    chips = ep_size // CORES
    tok, dim = hid.shape
    n_exp, _, inter = wg.shape
    top_k = ids.shape[0]
    half = dim // 2
    rows = ep_size * tok
    n_blk = dim // COLS
    hc = COLS // 2

    me = lax.axis_index("ep")
    chip, core = me // CORES, me % CORES
    other = 1 - core
    right, left, opp = (chip + 1) % chips, (chip + chips - 1) % chips, (chip + 2) % chips

    def slot(a_chip, a_core):
        return a_core * chips + a_chip

    def dev(a_chip, a_core):
        return {"ep": a_chip * CORES + a_core}

    used = [0]

    def remote(src, dst, to):
        i = used[0]
        used[0] += 1
        copy = pltpu.make_async_remote_copy(src, dst, send_sem.at[i], recv_sem.at[i], device_id=to, device_id_type=MESH)
        copy.start()
        sent.append(copy)
        return copy

    sent = []

    ins = [pltpu.make_async_copy(s, d, in_sem.at[i]) for i, (s, d) in enumerate(((hid_h, hid), (gain_h, gain), (rw_h, rw), (ids_h, ids)))]
    for copy in ins:
        copy.start()
    wcopies = {}

    def fetch(key, s, d):
        copy = pltpu.make_async_copy(s, d, w_sem.at[len(wcopies)])
        copy.start(priority=1)
        wcopies[key] = copy

    for e in range(n_exp):
        fetch(("g", e), wg_h.at[e], wg.at[e])
        fetch(("u", e), wu_h.at[e], wu.at[e])
    for e in range(n_exp):
        fetch(("d", e), wd_h.at[e], wd.at[e])
    fetch("sg", sg_h, sg)
    fetch("su", su_h, su)
    fetch("sd", sd_h, sd)

    barrier = pltpu.get_barrier_semaphore()
    for k in range(1, ep_size):
        pl.semaphore_signal(barrier, inc=1, device_id={"ep": (me + k) % ep_size}, device_id_type=MESH)

    mine = slot(chip, core)
    ins[0].wait()
    ins[1].wait()
    x_f32 = hid[...].astype(F32)
    inv_rms = lax.rsqrt(jnp.mean(x_f32 * x_f32, axis=-1, keepdims=True) + NORM_EPS)
    x_norm = (x_f32 * inv_rms * gain[...]).astype(BF16)
    x_all[mine] = x_norm

    pl.semaphore_wait(barrier, ep_size - 1)

    part_a, part_b = slice(0, half), slice(half, dim)

    def spread(a_slot, cols, to):
        ref = x_all.at[a_slot, :, cols]
        return remote(ref, ref, to)

    ra = spread(mine, part_a, dev(right, core))
    lb = spread(mine, part_b, dev(left, core))
    rb = spread(mine, part_b, dev(right, core))
    la = spread(mine, part_a, dev(left, core))
    cross = [spread(mine, slice(0, dim), dev(chip, other))]

    ins[2].wait()
    ins[3].wait()
    r_hi, r_mid, r_low = split3(rw[...])
    logits = (dot_t(r_low, x_norm) + dot_t(r_mid, x_norm)) + dot_t(r_hi, x_norm)
    scores = 1.0 / (1.0 + jnp.exp(-logits))
    exp_no = lax.broadcasted_iota(jnp.int32, logits.shape, 0)
    chosen = exp_no == ids[0:1, :]
    for k in range(1, top_k):
        chosen = jnp.logical_or(chosen, exp_no == ids[k : k + 1, :])
    total = jnp.sum(jnp.where(chosen, scores, 0.0), axis=0, keepdims=True)
    gates = jnp.where(chosen, ROUTE_SCALE * scores / total, -1.0)
    gt_send[...] = jnp.full(gt_send.shape, -1.0, F32)
    for d in range(ep_size):
        gt_send[d, :, 0:tok] = gates[d * n_exp : (d + 1) * n_exp, :]
    gt_all[mine] = gt_send[me]
    tiles = []
    for k in range(1, ep_size):
        to = (me + k) % ep_size
        tiles.append(remote(gt_send.at[to], gt_all.at[mine], {"ep": to}))

    ra.wait_recv()
    fa = spread(slot(left, core), part_a, dev(right, core))
    cross.append(spread(slot(left, core), part_a, dev(chip, other)))
    lb.wait_recv()
    fb = spread(slot(right, core), part_b, dev(left, core))
    cross.append(spread(slot(right, core), part_b, dev(chip, other)))
    rb.wait_recv()
    cross.append(spread(slot(left, core), part_b, dev(chip, other)))
    la.wait_recv()
    cross.append(spread(slot(right, core), part_a, dev(chip, other)))

    for copy in tiles:
        copy.wait_recv()
    lane_src = lax.broadcasted_iota(jnp.int32, (n_exp, rows), 1) // tok
    gmat = jnp.full((n_exp, rows), -1.0, F32)
    for s in range(ep_size):
        wide = jnp.concatenate([gt_all[s], jnp.full((n_exp, rows - gt_all.shape[2]), -1.0, F32)], axis=1)
        if s:
            wide = pltpu.roll(wide, s * tok, 1)
        gmat = jnp.where(lane_src == s, wide, gmat)
    picked = jnp.logical_not(gmat < 0.0)
    upper = lax.broadcasted_iota(jnp.int32, (rows, rows), 0) < lax.broadcasted_iota(jnp.int32, (rows, rows), 1)
    rank = dot(jnp.where(picked, 1.0, 0.0).astype(BF16), jnp.where(upper, 1.0, 0.0).astype(BF16))
    place = jnp.where(picked, rank, -1.0)
    row_no = lax.broadcasted_iota(jnp.int32, (cap, rows), 0).astype(F32)
    for e in range(n_exp):
        hit = row_no == place[e : e + 1, :]
        p_all[e * cap : (e + 1) * cap, :] = jnp.where(hit, 1.0, 0.0).astype(BF16)
        ga[e * cap : (e + 1) * cap, :] = jnp.where(hit, gmat[e : e + 1, :], 0.0)
    for i in range(n_exp * cap // 128):
        lanes = slice(i * 128, (i + 1) * 128)
        hi, mid, low = split3(ga[lanes, :].T)
        a_hi[:, lanes] = hi
        a_mid[:, lanes] = mid
        a_low[:, lanes] = low

    fa.wait_recv()
    cross.append(spread(slot(opp, core), part_a, dev(chip, other)))
    fb.wait_recv()
    cross.append(spread(slot(opp, core), part_b, dev(chip, other)))
    for copy in cross:
        copy.wait_recv()

    x_rows = x_all[...].reshape(rows, dim)
    for e in range(0, n_exp, 2):
        two = slice(e * cap, (e + 2) * cap)
        xg[two, :] = dot(p_all[two, :], x_rows).astype(BF16)
    for e in range(n_exp):
        own = slice(e * cap, (e + 1) * cap)
        wcopies[("g", e)].wait()
        wcopies[("u", e)].wait()
        h_gate = dot(xg[own, :], wg[e])
        h_up = dot(xg[own, :], wu[e])
        hbuf[own, :] = (jax.nn.silu(h_gate) * h_up).astype(BF16)
    for e in range(n_exp):
        wcopies[("d", e)].wait()

    part = []

    def compute(j):
        cols = slice(j * COLS, (j + 1) * COLS)
        for e in range(n_exp):
            own = slice(e * cap, (e + 1) * cap)
            ybuf[own, :] = dot(hbuf[own, :], wd[e, :, cols]).astype(BF16)
        y = ybuf[...]
        s = (dot(a_low[...], y) + dot(a_mid[...], y)) + dot(a_hi[...], y)
        sbuf[j] = s.reshape(CORES, chips * tok, COLS)
        part.append({"d2d": remote(sbuf.at[j, other], d2d.at[j], dev(chip, other))})

    lo, up = slice(0, hc), slice(hc, COLS)

    def send(j):
        part[j]["d2d"].wait_recv()
        tbuf[j] = (sbuf[j, core] + d2d[j]).reshape(chips, tok, COLS)
        part[j]["ha"] = remote(tbuf.at[j, opp, :, lo], hopa.at[j], dev(right, core))
        part[j]["hb"] = remote(tbuf.at[j, opp, :, up], hopb.at[j], dev(left, core))
        part[j]["db"] = remote(tbuf.at[j, right, :, up], froml.at[j, :, up], dev(right, core))
        part[j]["da"] = remote(tbuf.at[j, left, :, lo], fromr.at[j, :, lo], dev(left, core))

    def relay(j):
        part[j]["ha"].wait_recv()
        rela[j] = hopa[j] + tbuf[j, right, :, lo]
        part[j]["ra"] = remote(rela.at[j], froml.at[j, :, lo], dev(right, core))
        part[j]["hb"].wait_recv()
        relb[j] = hopb[j] + tbuf[j, left, :, up]
        part[j]["rb"] = remote(relb.at[j], fromr.at[j, :, up], dev(left, core))

    def finish(j):
        for key in ("db", "da", "ra", "rb"):
            part[j][key].wait_recv()
        cols = slice(j * COLS, (j + 1) * COLS)
        routed = (tbuf[j, chip] + froml[j]) + fromr[j]
        out_ref[:, cols] = ((hid[:, cols].astype(F32) + shared[:, cols].astype(F32)) + routed).astype(BF16)

    for j in range(n_blk):
        compute(j)
        if j >= 1:
            send(j - 1)
        if j >= 3:
            relay(j - 3)
    send(n_blk - 1)
    relay(n_blk - 3)

    wcopies["sg"].wait()
    wcopies["su"].wait()
    wcopies["sd"].wait()
    xs = x_all[mine]
    mid_cols = hsh.shape[1] // 2
    for k in range(2):
        cols = slice(k * mid_cols, (k + 1) * mid_cols)
        hsh[:, cols] = (jax.nn.silu(dot(xs, sg[:, cols])) * dot(xs, su[:, cols])).astype(BF16)
        relay(n_blk - 2 + k)
    shared[...] = dot(hsh[...], sd[...]).astype(BF16)
    for j in range(n_blk):
        finish(j)
    for copy in sent:
        copy.wait_send()


def solution(mesh):
    ep_size = mesh.shape["ep"]

    def local_block(hidden_in, norm_gain, router_w, w_gate, w_up, w_down, ws_gate, ws_up, ws_down, expert_ids):
        tok, top_k = expert_ids.shape
        dim = hidden_in.shape[1]
        n_exp, _, inter = w_gate.shape
        s_inter = ws_gate.shape[1]
        cap = GROUPS * ((top_k + GROUP_LIMIT - 1) // GROUP_LIMIT) * tok // n_exp
        rows = ep_size * tok
        pairs = n_exp * cap
        n_blk = dim // COLS
        chips = ep_size // CORES
        vm = pltpu.VMEM
        n_remote = 6 + 7 + (ep_size - 1) + 7 * n_blk
        scratch = [
            vm((tok, dim), BF16), vm((1, dim), F32), vm(router_w.shape, F32), vm((top_k, tok), jnp.int32),
            vm(w_gate.shape, BF16), vm(w_up.shape, BF16), vm(w_down.shape, BF16),
            vm(ws_gate.shape, BF16), vm(ws_up.shape, BF16), vm(ws_down.shape, BF16),
            vm((ep_size, tok, dim), BF16), vm((ep_size, n_exp, 128), F32), vm((ep_size, n_exp, 128), F32),
            vm((pairs, rows), BF16), vm((pairs, rows), F32),
            vm((rows, pairs), BF16), vm((rows, pairs), BF16), vm((rows, pairs), BF16),
            vm((pairs, dim), BF16), vm((pairs, inter), BF16), vm((pairs, COLS), BF16),
            vm((n_blk, CORES, chips * tok, COLS), F32), vm((n_blk, chips * tok, COLS), F32), vm((n_blk, chips, tok, COLS), F32),
            vm((n_blk, tok, COLS // 2), F32), vm((n_blk, tok, COLS // 2), F32), vm((n_blk, tok, COLS // 2), F32), vm((n_blk, tok, COLS // 2), F32),
            vm((n_blk, tok, COLS), F32), vm((n_blk, tok, COLS), F32),
            vm((tok, s_inter), BF16), vm((tok, dim), BF16),
            pltpu.SemaphoreType.DMA((4,)), pltpu.SemaphoreType.DMA((3 * n_exp + 3,)),
            pltpu.SemaphoreType.DMA((n_remote,)), pltpu.SemaphoreType.DMA((n_remote,)),
        ]
        return pl.pallas_call(
            functools.partial(moe_kernel, ep_size, cap),
            out_shape=jax.ShapeDtypeStruct((tok, dim), BF16),
            in_specs=[pl.BlockSpec(memory_space=pl.ANY)] * 10,
            out_specs=pl.BlockSpec(memory_space=pltpu.VMEM),
            scratch_shapes=scratch,
            compiler_params=pltpu.CompilerParams(collective_id=0, has_side_effects=True, vmem_limit_bytes=67_000_000),
            name="moe_block",
        )(hidden_in, norm_gain[None, :], router_w, w_gate, w_up, w_down, ws_gate, ws_up, ws_down, expert_ids.T)

    row_spec = P(("dp", "ep"), None)
    in_specs = (row_spec, P(), P(), P("ep"), P("ep"), P("ep"), P(), P(), P(), row_spec)
    return jax.shard_map(local_block, mesh=mesh, in_specs=in_specs, out_specs=row_spec, check_vma=False)
```

time: 154 us -> 42.5 us (0.28)
  waiting for transfers between devices: 44.6 us -> 0 us
  local copies, waits for them, and re-layouts: 45.2 us -> 2.87 us
  Pallas kernels: 0 us -> 39.5 us
  matrix products: 30.6 us -> 0 us
  other arithmetic: 17.6 us -> 0 us
  starting transfers between devices: 15 us -> 0 us
    all_to_all x3 -> x0, waiting for transfers between devices: 44.6 us -> none  [the longest x1 22.5 us: local_block(): recv_rows = lax.all_to_all(send_rows, 'ep', 0, 0, tiled=True)]
    pallas_call x0 -> x1, Pallas kernels: none -> 39.5 us  [local_block(): pl.pallas_call(functools.partial(moe_kernel, ep_size, cap), out_shape=jax...]
    gather x10 -> x0, local copies, waits for them, and re-layouts: 30.8 us -> none  [the longest x2 8.34 us: local_block(): jnp.take(returned, send_slot, axis=0).reshape(tok_dev, top_k, model_dim)]
    dot_general x5 -> x0, matrix products: 30.6 us -> none  [the longest x1 14.9 us: expert_stack(): jnp.einsum('eci,eid->ecd', hidden, w_down, preferred_element_type=jnp.flo...]
    all_to_all x3 -> x0, starting transfers between devices: 15 us -> none  [the longest x1 5.3 us: local_block(): recv_exp = lax.all_to_all(slot_exp, 'ep', 0, 0, tiled=True)]
    scatter x3 -> x0, local copies, waits for them, and re-layouts: 9.4 us -> none  [the longest x1 3.56 us: local_block(): jnp.full((recv_cap,), recv_cap, jnp.int32).at[buf_slot]]
    select_n x9 -> x0, other arithmetic: 8.55 us -> none  [the longest x2 3.29 us: local_block(): send_rows = jnp.take(x_norm, slot_tok, axis=0, mode='fill', fill_value=0)]
    reduce_sum x5 -> x0, other arithmetic: 4.36 us -> none  [the longest x1 3.18 us: local_block(): jnp.sum(gate_vals[:, :, None] * pair_out.astype(jnp.float32), axis=1)]
  transfers between devices with their start and end apart: 3 -> 0, of which waited for: 2 -> 0; matrix products, arithmetic and copies ran while one was open for 18% -> 0% of each run, Pallas kernels for 0% -> 0%
where the time goes in v1:
time: 42.5 us; the launch traced here: 42.4 us
  Pallas kernels  39.5 us (93%)
  local copies, waits for them, and re-layouts  2.87 us (7%)
    pallas_call x1, Pallas kernels, local_block(): pl.pallas_call(functools.partial(moe_kernel, ep_size, cap), out_shape=jax...  39.5 us
    unnamed x1, local copies, waits for them, and re-layouts  1.58 us
    broadcast_in_dim x1, local copies, waits for them, and re-layouts, local_block(): norm_gain[None, :]  1.29 us

profile of v1, /device:TPU:112, one launch (start us, length us, event | category | flops | bytes accessed | tf_op | source)
XLA Modules:
  0.0 42.4 jit_solution(4161195938830798794)
XLA Ops:
  0.0 1.3 %broadcast_in_dim.3.gain_h = f32[1,1536]{1,0:T(1,128)} reshape(f32[1536]{0:T(1024)} %param.11) | data formatting | bytes 12288 | tf_op jit(solution)/shard_map/broadcast_in_dim | solution.py:295
  1.3 39.5 %moe_block.1 = bf16[48,1536]{1,0:T(8,128)(2,1)} custom-call(bf16[48,1536]{1,0:T(8,128)(2,1)} %hid_h.1, f32[1,1536]{1,0:T(1,128)} %broadcast_in_dim.3.gain_h, f32[64,1536]{1,0:T(8,128)} %rw_h.1, bf16[8,1536,512]{2,1,0:T(8,128)(2,1)} %wg_h.1, bf16[8,1536,512]{2,1,0:T(8,128)(2,1)} %wu_h.1, bf16[8,512,1536]{2,1,0:T(8,128)(2,1)} %wd_h.1, ...), custom_call_target="tpu_custom_call" | custom-call | tf_op jit(solution)/shard_map/moe_block/pallas_call | solution.py:287
  40.8 1.6 %copy.12 = bf16[48,1536]{1,0:T(8,128)(2,1)} copy(bf16[48,1536]{1,0:T(8,128)(2,1)} %moe_block.1) | data formatting | bytes 294912

commit v2 on v0

v2 whole, which is shorter than its diff:
```python
import functools

import jax
import jax.numpy as jnp
from jax import lax
from jax.experimental import pallas as pl
from jax.experimental.pallas import tpu as pltpu
from jax.sharding import PartitionSpec as P

NORM_EPS = 1e-6
ROUTE_SCALE = 2.5
GROUPS = 8
GROUP_LIMIT = 4
CORES = 2
COLS = 256
MESH = pl.DeviceIdType.MESH
F32 = jnp.float32
BF16 = jnp.bfloat16


def dot(a, b):
    return jnp.dot(a, b, preferred_element_type=F32)


def dot_t(a, b):
    return lax.dot_general(a, b, (((1,), (1,)), ((), ())), preferred_element_type=F32)


def split3(v):
    hi = v.astype(BF16)
    rest = v - hi.astype(F32)
    mid = rest.astype(BF16)
    low = (rest - mid.astype(F32)).astype(BF16)
    return hi, mid, low


def moe_kernel(ep_size, cap, hid_h, gain_h, rw_h, wg_h, wu_h, wd_h, sg_h, su_h, sd_h, ids_h, out_ref,
               hid, gain, rw, ids, wg, wu, wd, sg, su, sd, x_all, gt_send, gt_all, p_all, ga, acat,
               xg, hbuf, ybuf, sbuf, d2d, tbuf, hop, rel, froml, fromr, hsh, shared,
               obuf, in_sem, w_sem, o_sem,
               ring_s, cross_s, tile_s, d2d_s, hop_s, dir_s, rel_s, ag_r, cross_r, tile_r, d2d_r, hop_r, end_r):
    chips = ep_size // CORES
    tok, dim = hid.shape
    n_exp, _, inter = wg.shape
    top_k = ids.shape[0]
    half = dim // 2
    rows = ep_size * tok
    n_blk = dim // COLS
    hc = COLS // 2
    pairs = n_exp * cap

    me = lax.axis_index("ep")
    chip, core = me // CORES, me % CORES
    other = 1 - core
    right, left, opp = (chip + 1) % chips, (chip + chips - 1) % chips, (chip + 2) % chips

    def slot(a_chip, a_core):
        return a_core * chips + a_chip

    def dev(a_chip, a_core):
        return {"ep": a_chip * CORES + a_core}

    def remote(src, dst, to, s_sem, r_sem):
        copy = pltpu.make_async_remote_copy(src, dst, s_sem, r_sem, device_id=to, device_id_type=MESH)
        copy.start()
        return copy

    def await_all(ref, sem):
        pltpu.make_async_copy(ref, ref, sem).wait()

    ins = [pltpu.make_async_copy(s, d, in_sem.at[i]) for i, (s, d) in enumerate(((hid_h, hid), (gain_h, gain), (rw_h, rw), (ids_h, ids)))]
    for copy in ins:
        copy.start()
    weights = []
    for i, (s, d) in enumerate(((wg_h, wg), (wu_h, wu), (wd_h, wd), (sg_h, sg), (su_h, su), (sd_h, sd))):
        weights.append(pltpu.make_async_copy(s, d, w_sem.at[i]))
        weights[-1].start(priority=1)

    barrier = pltpu.get_barrier_semaphore()
    for k in range(1, ep_size):
        pl.semaphore_signal(barrier, inc=1, device_id={"ep": (me + k) % ep_size}, device_id_type=MESH)

    mine = slot(chip, core)
    with jax.named_scope("norm"):
        ins[0].wait()
        ins[1].wait()
        x_f32 = hid[...].astype(F32)
        inv_rms = lax.rsqrt(jnp.mean(x_f32 * x_f32, axis=-1, keepdims=True) + NORM_EPS)
        gain_row = jnp.concatenate([gain[i : i + 1, :] for i in range(dim // 128)], axis=1)
        x_norm = (x_f32 * inv_rms * gain_row).astype(BF16)
        x_all[mine] = x_norm

    with jax.named_scope("barwait"):
        pl.semaphore_wait(barrier, ep_size - 1)

    quarter = half // 2
    q = [slice(k * quarter, (k + 1) * quarter) for k in range(4)]
    part_a, part_b = slice(0, half), slice(half, dim)

    def spread(a_slot, cols, to, r_sem):
        ref = x_all.at[a_slot, :, cols]
        return remote(ref, ref, to, ring_s, r_sem)

    def cross(a_slot, cols):
        ref = x_all.at[a_slot, :, cols]
        remote(ref, ref, dev(chip, other), cross_s, cross_r)

    ra = [spread(mine, q[k], dev(right, core), ag_r.at[k]) for k in range(2)]
    lb = [spread(mine, q[2 + k], dev(left, core), ag_r.at[2 + k]) for k in range(2)]
    rb = spread(mine, part_b, dev(right, core), ag_r.at[4])
    la = spread(mine, part_a, dev(left, core), ag_r.at[5])
    cross(mine, slice(0, dim))

    with jax.named_scope("router"):
        ins[2].wait()
        ins[3].wait()
        r_hi, r_mid, r_low = split3(rw[...])
        logits = (dot_t(r_low, x_norm) + dot_t(r_mid, x_norm)) + dot_t(r_hi, x_norm)
        scores = 1.0 / (1.0 + jnp.exp(-logits))
        exp_no = lax.broadcasted_iota(jnp.int32, logits.shape, 0)
        chosen = exp_no == ids[0:1, :]
        for k in range(1, top_k):
            chosen = jnp.logical_or(chosen, exp_no == ids[k : k + 1, :])
        total = jnp.sum(jnp.where(chosen, scores, 0.0), axis=0, keepdims=True)
        gates = jnp.where(chosen, ROUTE_SCALE * scores / total, -1.0)
        gt_send[...] = jnp.full(gt_send.shape, -1.0, F32)
        for d in range(ep_size):
            gt_send[d, :, 0:tok] = gates[d * n_exp : (d + 1) * n_exp, :]
        gt_all[mine] = gt_send[me]
        for k in range(1, ep_size):
            to = (me + k) % ep_size
            remote(gt_send.at[to], gt_all.at[mine], {"ep": to}, tile_s, tile_r)

    with jax.named_scope("relays"):
        for k in range(2):
            ra[k].wait_recv()
            spread(slot(left, core), q[k], dev(right, core), ag_r.at[6])
            cross(slot(left, core), q[k])
            lb[k].wait_recv()
            spread(slot(right, core), q[2 + k], dev(left, core), ag_r.at[7])
            cross(slot(right, core), q[2 + k])
        rb.wait_recv()
        cross(slot(left, core), part_b)
        la.wait_recv()
        cross(slot(right, core), part_a)

    with jax.named_scope("tilewait"):
        await_all(gt_all.at[0 : ep_size - 1], tile_r)

    with jax.named_scope("onehot"):
        lane_src = lax.broadcasted_iota(jnp.int32, (n_exp, rows), 1) // tok
        gmat = jnp.full((n_exp, rows), -1.0, F32)
        for s in range(ep_size):
            wide = jnp.concatenate([gt_all[s], jnp.full((n_exp, rows - gt_all.shape[2]), -1.0, F32)], axis=1)
            if s:
                wide = pltpu.roll(wide, s * tok, 1)
            gmat = jnp.where(lane_src == s, wide, gmat)
        picked = jnp.logical_not(gmat < 0.0)
        upper = lax.broadcasted_iota(jnp.int32, (rows, rows), 0) < lax.broadcasted_iota(jnp.int32, (rows, rows), 1)
        rank = dot(jnp.where(picked, 1.0, 0.0).astype(BF16), jnp.where(upper, 1.0, 0.0).astype(BF16))
        place = jnp.where(picked, rank, -1.0)
        row_no = lax.broadcasted_iota(jnp.int32, (cap, rows), 0).astype(F32)
        for e in range(n_exp):
            hit = row_no == place[e : e + 1, :]
            p_all[e * cap : (e + 1) * cap, :] = jnp.where(hit, 1.0, 0.0).astype(BF16)
            ga[e * cap : (e + 1) * cap, :] = jnp.where(hit, gmat[e : e + 1, :], 0.0)
        for i in range(n_exp * cap // 128):
            lanes = slice(i * 128, (i + 1) * 128)
            hi, mid, low = split3(ga[lanes, :].T)
            for k, term in enumerate((low, mid, hi)):
                acat[:, k * pairs + i * 128 : k * pairs + (i + 1) * 128] = term

    with jax.named_scope("agwait"):
        await_all(x_all.at[slot(opp, core), :, part_a], ag_r.at[6])
        cross(slot(opp, core), part_a)
        await_all(x_all.at[slot(opp, core), :, part_b], ag_r.at[7])
        cross(slot(opp, core), part_b)
        await_all(x_all.at[pl.ds(other * chips, chips)], cross_r)

    with jax.named_scope("wwait"):
        weights[0].wait()
        weights[1].wait()

    with jax.named_scope("gateup"):
        x_rows = x_all[...].reshape(rows, dim)

        def gather(e):
            xg[(e // 2) % 2] = dot(p_all[e * cap : (e + 2) * cap, :], x_rows).astype(BF16)

        gather(0)
        for e in range(n_exp):
            if e % 2 == 0 and e + 2 < n_exp:
                gather(e + 2)
            xe = xg[(e // 2) % 2, (e % 2) * cap : (e % 2 + 1) * cap, :]
            h_gate = dot(xe, wg[e])
            h_up = dot(xe, wu[e])
            hbuf[e * cap : (e + 1) * cap, :] = (jax.nn.silu(h_gate) * h_up).astype(BF16)

    with jax.named_scope("dwait"):
        weights[2].wait()

    part = []

    def last(j):
        cols = slice(j * COLS, (j + 1) * COLS)
        for e in range(n_exp):
            y = dot(hbuf[e * cap : (e + 1) * cap, :], wd[e, :, cols]).astype(BF16)
            for k in range(3):
                ybuf[j % 2, k * pairs + e * cap : k * pairs + (e + 1) * cap, :] = y

    def compute(j):
        if j == 1:
            last(1)
        if j and j + 1 < n_blk:
            last(j + 1)
        for k in range(CORES):
            sbuf[j, k] = dot(acat[k * chips * tok : (k + 1) * chips * tok, :], ybuf[j % 2])
        part.append(remote(sbuf.at[j, other], d2d.at[j], dev(chip, other), d2d_s, d2d_r.at[j]))

    lo, up = slice(0, hc), slice(hc, COLS)
    half_blk = n_blk // 2

    def send(j):
        part[j].wait_recv()
        tbuf[j] = (sbuf[j, core] + d2d[j]).reshape(chips, tok, COLS)
        remote(tbuf.at[j, opp, :, lo], hop.at[j, :, lo], dev(right, core), hop_s, hop_r.at[j])
        remote(tbuf.at[j, opp, :, up], hop.at[j, :, up], dev(left, core), hop_s, hop_r.at[j])

    def direct(j):
        remote(tbuf.at[j, right, :, up], froml.at[j, :, up], dev(right, core), dir_s, end_r.at[0, j // half_blk])
        remote(tbuf.at[j, left, :, lo], fromr.at[j, :, lo], dev(left, core), dir_s, end_r.at[1, j // half_blk])

    def relay(j):
        await_all(hop.at[j], hop_r.at[j])
        rel[j, :, lo] = hop[j, :, lo] + tbuf[j, right, :, lo]
        rel[j, :, up] = hop[j, :, up] + tbuf[j, left, :, up]
        remote(rel.at[j, :, lo], froml.at[j, :, lo], dev(right, core), rel_s, end_r.at[0, j // half_blk])
        remote(rel.at[j, :, up], fromr.at[j, :, up], dev(left, core), rel_s, end_r.at[1, j // half_blk])

    def finish(k):
        blks = slice(k * half_blk, (k + 1) * half_blk)
        await_all(froml.at[blks], end_r.at[0, k])
        await_all(fromr.at[blks], end_r.at[1, k])
        for j in range(k * half_blk, (k + 1) * half_blk):
            cols = slice(j * COLS, (j + 1) * COLS)
            routed = (tbuf[j, chip] + froml[j]) + fromr[j]
            obuf[:, cols] = ((hid[:, cols].astype(F32) + shared[:, cols].astype(F32)) + routed).astype(BF16)
        cols = slice(k * half_blk * COLS, (k + 1) * half_blk * COLS)
        pltpu.make_async_copy(obuf.at[:, cols], out_ref.at[:, cols], o_sem).start()

    def scoped(f, j):
        with jax.named_scope(f"{f.__name__}{j}"):
            f(j)

    last(0)
    for j in range(n_blk):
        scoped(compute, j)
        if j >= 1:
            scoped(send, j - 1)
            scoped(direct, j - 1)
    scoped(send, n_blk - 1)

    with jax.named_scope("shared"):
        for copy in weights[3:]:
            copy.wait()
        xs = x_all[mine]
        mid_cols = hsh.shape[1] // 2

        def shared_part(k):
            cols = slice(k * mid_cols, (k + 1) * mid_cols)
            hsh[:, cols] = (jax.nn.silu(dot(xs, sg[:, cols])) * dot(xs, su[:, cols])).astype(BF16)

        scoped(relay, 0)
        scoped(relay, 1)
        scoped(direct, n_blk - 1)
        shared_part(0)
        scoped(relay, 2)
        scoped(relay, 3)
        shared_part(1)
        scoped(relay, 4)
        scoped(relay, 5)
        shared[...] = dot(hsh[...], sd[...]).astype(BF16)
    for k in range(2):
        scoped(finish, k)
    with jax.named_scope("drain"):
        await_all(x_all.at[0:3], ring_s)
        await_all(x_all.at[0:chips], cross_s)
        await_all(gt_send.at[0 : ep_size - 1], tile_s)
        await_all(d2d, d2d_s)
        await_all(hop, hop_s)
        await_all(froml, dir_s)
        await_all(rel, rel_s)
        pltpu.make_async_copy(obuf, out_ref, o_sem).wait()


def solution(mesh):
    ep_size = mesh.shape["ep"]

    def local_block(hidden_in, norm_gain, router_w, w_gate, w_up, w_down, ws_gate, ws_up, ws_down, expert_ids):
        tok, top_k = expert_ids.shape
        dim = hidden_in.shape[1]
        n_exp, _, inter = w_gate.shape
        s_inter = ws_gate.shape[1]
        cap = GROUPS * ((top_k + GROUP_LIMIT - 1) // GROUP_LIMIT) * tok // n_exp
        rows = ep_size * tok
        pairs = n_exp * cap
        n_blk = dim // COLS
        chips = ep_size // CORES
        vm, sem = pltpu.VMEM, pltpu.SemaphoreType.DMA
        scratch = [
            vm((tok, dim), BF16), vm((dim // 128, 128), F32), vm(router_w.shape, F32), vm((top_k, tok), jnp.int32),
            vm(w_gate.shape, BF16), vm(w_up.shape, BF16), vm(w_down.shape, BF16),
            vm(ws_gate.shape, BF16), vm(ws_up.shape, BF16), vm(ws_down.shape, BF16),
            vm((ep_size, tok, dim), BF16), vm((ep_size, n_exp, 128), F32), vm((ep_size, n_exp, 128), F32),
            vm((pairs, rows), BF16), vm((pairs, rows), F32),
            vm((rows, 3 * pairs), BF16),
            vm((2, 2 * cap, dim), BF16), vm((pairs, inter), BF16), vm((2, 3 * pairs, COLS), BF16),
            vm((n_blk, CORES, chips * tok, COLS), F32), vm((n_blk, chips * tok, COLS), F32), vm((n_blk, chips, tok, COLS), F32),
            vm((n_blk, tok, COLS), F32), vm((n_blk, tok, COLS), F32), vm((n_blk, tok, COLS), F32), vm((n_blk, tok, COLS), F32),
            vm((tok, s_inter), BF16), vm((tok, dim), BF16), vm((tok, dim), BF16),
            sem((4,)), sem((6,)), sem, sem, sem, sem, sem, sem, sem, sem,
            sem((8,)), sem, sem, sem((n_blk,)), sem((n_blk,)), sem((2, 2)),
        ]
        return pl.pallas_call(
            functools.partial(moe_kernel, ep_size, cap),
            out_shape=jax.ShapeDtypeStruct((tok, dim), BF16),
            in_specs=[pl.BlockSpec(memory_space=pl.ANY)] * 10,
            out_specs=pl.BlockSpec(memory_space=pl.ANY),
            scratch_shapes=scratch,
            compiler_params=pltpu.CompilerParams(collective_id=0, has_side_effects=True, vmem_limit_bytes=67_000_000),
            name="moe_block",
        )(hidden_in, norm_gain.reshape(dim // 128, 128), router_w, w_gate, w_up, w_down, ws_gate, ws_up, ws_down, expert_ids.T)

    row_spec = P(("dp", "ep"), None)
    in_specs = (row_spec, P(), P(), P("ep"), P("ep"), P("ep"), P(), P(), P(), row_spec)
    return jax.shard_map(local_block, mesh=mesh, in_specs=in_specs, out_specs=row_spec, check_vma=False)
```

time: 154 us -> 35.7 us (0.23)
  waiting for transfers between devices: 44.6 us -> 0 us
  local copies, waits for them, and re-layouts: 45.2 us -> 1.58 us
  Pallas kernels: 0 us -> 34 us
  matrix products: 30.6 us -> 0 us
  other arithmetic: 17.6 us -> 0 us
  starting transfers between devices: 15 us -> 0 us
    all_to_all x3 -> x0, waiting for transfers between devices: 44.6 us -> none  [the longest x1 22.5 us: local_block(): recv_rows = lax.all_to_all(send_rows, 'ep', 0, 0, tiled=True)]
    pallas_call x0 -> x1, Pallas kernels: none -> 34 us  [local_block(): pl.pallas_call(functools.partial(moe_kernel, ep_size, cap), out_shape=jax...]
    gather x10 -> x0, local copies, waits for them, and re-layouts: 30.8 us -> none  [the longest x2 8.34 us: local_block(): jnp.take(returned, send_slot, axis=0).reshape(tok_dev, top_k, model_dim)]
    dot_general x5 -> x0, matrix products: 30.6 us -> none  [the longest x1 14.9 us: expert_stack(): jnp.einsum('eci,eid->ecd', hidden, w_down, preferred_element_type=jnp.flo...]
    all_to_all x3 -> x0, starting transfers between devices: 15 us -> none  [the longest x1 5.3 us: local_block(): recv_exp = lax.all_to_all(slot_exp, 'ep', 0, 0, tiled=True)]
    scatter x3 -> x0, local copies, waits for them, and re-layouts: 9.4 us -> none  [the longest x1 3.56 us: local_block(): jnp.full((recv_cap,), recv_cap, jnp.int32).at[buf_slot]]
    select_n x9 -> x0, other arithmetic: 8.55 us -> none  [the longest x2 3.29 us: local_block(): send_rows = jnp.take(x_norm, slot_tok, axis=0, mode='fill', fill_value=0)]
    reduce_sum x5 -> x0, other arithmetic: 4.36 us -> none  [the longest x1 3.18 us: local_block(): jnp.sum(gate_vals[:, :, None] * pair_out.astype(jnp.float32), axis=1)]
  transfers between devices with their start and end apart: 3 -> 0, of which waited for: 2 -> 0; matrix products, arithmetic and copies ran while one was open for 18% -> 0% of each run, Pallas kernels for 0% -> 0%
where the time goes in v2:
time: 35.7 us; the launch traced here: 35.6 us
  Pallas kernels  34 us (95%)
  local copies, waits for them, and re-layouts  1.58 us (4%)
    pallas_call x1, Pallas kernels, local_block(): pl.pallas_call(functools.partial(moe_kernel, ep_size, cap), out_shape=jax...  34 us
    unnamed x1, local copies, waits for them, and re-layouts  1.58 us

profile of v2, /device:TPU:112, one launch (start us, length us, event | category | flops | bytes accessed | tf_op | source)
XLA Modules:
  0.0 35.6 jit_solution(12482323495792949614)
XLA Ops:
  0.0 34.0 %moe_block.1 = bf16[48,1536]{1,0:T(8,128)(2,1)} custom-call(bf16[48,1536]{1,0:T(8,128)(2,1)} %hid_h.1, f32[12,128]{1,0:T(8,128)} %bitcast.2, f32[64,1536]{1,0:T(8,128)} %rw_h.1, bf16[8,1536,512]{2,1,0:T(8,128)(2,1)} %wg_h.1, bf16[8,1536,512]{2,1,0:T(8,128)(2,1)} %wu_h.1, bf16[8,512,1536]{2,1,0:T(8,128)(2,1)} %wd_h.1, bf16[1536,1024]{1,0:T(8,128)(2,1)} %sg_h.1, ...), custom_call_target="tpu_custom_call" | custom-call | tf_op jit(solution)/shard_map/moe_block/pallas_call | solution.py:324
  34.0 1.6 %copy.12 = bf16[48,1536]{1,0:T(8,128)(2,1)} copy(bf16[48,1536]{1,0:T(8,128)(2,1)} %moe_block.1) | data formatting | bytes 294912

commit v3 on v2

--- a/solution.py
+++ b/solution.py
@@ -12,6 +12,7 @@
 GROUPS = 8
 GROUP_LIMIT = 4
 CORES = 2
+POS_OWN, POS_RIGHT, POS_LEFT, POS_FAR = range(4)
 COLS = 256
 MESH = pl.DeviceIdType.MESH
 F32 = jnp.float32
@@ -35,9 +36,9 @@
 
 
 def moe_kernel(ep_size, cap, hid_h, gain_h, rw_h, wg_h, wu_h, wd_h, sg_h, su_h, sd_h, ids_h, out_ref,
-               hid, gain, rw, ids, wg, wu, wd, sg, su, sd, x_all, gt_send, gt_all, p_all, ga, acat,
+               hid, gain, rw, ids, wg, wu, wd, sg, su, sd, x_all, gt_send, gt_all, p_all, acat,
                xg, hbuf, ybuf, sbuf, d2d, tbuf, hop, rel, froml, fromr, hsh, shared,
-               obuf, in_sem, w_sem, o_sem,
+               in_sem, w_sem,
                ring_s, cross_s, tile_s, d2d_s, hop_s, dir_s, rel_s, ag_r, cross_r, tile_r, d2d_r, hop_r, end_r):
     chips = ep_size // CORES
     tok, dim = hid.shape
@@ -54,8 +55,9 @@
     other = 1 - core
     right, left, opp = (chip + 1) % chips, (chip + chips - 1) % chips, (chip + 2) % chips
 
-    def slot(a_chip, a_core):
-        return a_core * chips + a_chip
+    def slot(a_chip, a_core, at=None):
+        away = (a_chip - (chip if at is None else at) + chips) % chips
+        return (away + away // 2 - 2 * (away // 3)) * CORES + a_core
 
     def dev(a_chip, a_core):
         return {"ep": a_chip * CORES + a_core}
@@ -71,8 +73,10 @@
     ins = [pltpu.make_async_copy(s, d, in_sem.at[i]) for i, (s, d) in enumerate(((hid_h, hid), (gain_h, gain), (rw_h, rw), (ids_h, ids)))]
     for copy in ins:
         copy.start()
+    early, late = slice(0, COLS), slice(COLS, dim)
+    fetches = ((wg_h, wg), (wu_h, wu), (wd_h.at[:, :, early], wd.at[:, :, early]), (wd_h.at[:, :, late], wd.at[:, :, late]), (sg_h, sg), (su_h, su), (sd_h, sd))
     weights = []
-    for i, (s, d) in enumerate(((wg_h, wg), (wu_h, wu), (wd_h, wd), (sg_h, sg), (su_h, su), (sd_h, sd))):
+    for i, (s, d) in enumerate(fetches):
         weights.append(pltpu.make_async_copy(s, d, w_sem.at[i]))
         weights[-1].start(priority=1)
 
@@ -93,23 +97,22 @@
     with jax.named_scope("barwait"):
         pl.semaphore_wait(barrier, ep_size - 1)
 
-    quarter = half // 2
-    q = [slice(k * quarter, (k + 1) * quarter) for k in range(4)]
+    half = dim // 2
+    q = [slice(k * half // 2, (k + 1) * half // 2) for k in range(4)]
     part_a, part_b = slice(0, half), slice(half, dim)
 
-    def spread(a_slot, cols, to, r_sem):
-        ref = x_all.at[a_slot, :, cols]
-        return remote(ref, ref, to, ring_s, r_sem)
-
-    def cross(a_slot, cols):
-        ref = x_all.at[a_slot, :, cols]
-        remote(ref, ref, dev(chip, other), cross_s, cross_r)
-
-    ra = [spread(mine, q[k], dev(right, core), ag_r.at[k]) for k in range(2)]
-    lb = [spread(mine, q[2 + k], dev(left, core), ag_r.at[2 + k]) for k in range(2)]
-    rb = spread(mine, part_b, dev(right, core), ag_r.at[4])
-    la = spread(mine, part_a, dev(left, core), ag_r.at[5])
-    cross(mine, slice(0, dim))
+    def spread(a_chip, cols, to, r_sem):
+        src, dst = x_all.at[slot(a_chip, core), :, cols], x_all.at[slot(a_chip, core, to), :, cols]
+        return remote(src, dst, dev(to, core), ring_s, r_sem)
+
+    def cross(a_chip, cols, r_sem):
+        ref = x_all.at[slot(a_chip, core), :, cols]
+        remote(ref, ref, dev(chip, other), cross_s, r_sem)
+
+    ra, lb = [], []
+    for k in range(2):
+        ra.append(spread(chip, q[k], right, ag_r.at[k]))
+        lb.append(spread(chip, q[2 + k], left, ag_r.at[2 + k]))
 
     with jax.named_scope("router"):
         ins[2].wait()
@@ -129,20 +132,26 @@
         gt_all[mine] = gt_send[me]
         for k in range(1, ep_size):
             to = (me + k) % ep_size
-            remote(gt_send.at[to], gt_all.at[mine], {"ep": to}, tile_s, tile_r)
+            remote(gt_send.at[to], gt_all.at[slot(chip, core, to // CORES)], {"ep": to}, tile_s, tile_r)
+
+    rb = spread(chip, part_b, right, ag_r.at[4])
+    la = spread(chip, part_a, left, ag_r.at[5])
+    cross(chip, slice(0, dim), cross_r.at[0])
 
     with jax.named_scope("relays"):
         for k in range(2):
             ra[k].wait_recv()
-            spread(slot(left, core), q[k], dev(right, core), ag_r.at[6])
-            cross(slot(left, core), q[k])
+            spread(left, q[k], right, ag_r.at[6])
+            cross(left, q[k], cross_r.at[0])
             lb[k].wait_recv()
-            spread(slot(right, core), q[2 + k], dev(left, core), ag_r.at[7])
-            cross(slot(right, core), q[2 + k])
+            spread(right, q[2 + k], left, ag_r.at[7])
+            cross(right, q[2 + k], cross_r.at[0])
+
+    def near_rest():
         rb.wait_recv()
-        cross(slot(left, core), part_b)
+        cross(left, part_b, cross_r.at[0])
         la.wait_recv()
-        cross(slot(right, core), part_a)
+        cross(right, part_a, cross_r.at[0])
 
     with jax.named_scope("tilewait"):
         await_all(gt_all.at[0 : ep_size - 1], tile_r)
@@ -159,45 +168,44 @@
         upper = lax.broadcasted_iota(jnp.int32, (rows, rows), 0) < lax.broadcasted_iota(jnp.int32, (rows, rows), 1)
         rank = dot(jnp.where(picked, 1.0, 0.0).astype(BF16), jnp.where(upper, 1.0, 0.0).astype(BF16))
         place = jnp.where(picked, rank, -1.0)
-        row_no = lax.broadcasted_iota(jnp.int32, (cap, rows), 0).astype(F32)
-        for e in range(n_exp):
-            hit = row_no == place[e : e + 1, :]
-            p_all[e * cap : (e + 1) * cap, :] = jnp.where(hit, 1.0, 0.0).astype(BF16)
-            ga[e * cap : (e + 1) * cap, :] = jnp.where(hit, gmat[e : e + 1, :], 0.0)
-        for i in range(n_exp * cap // 128):
-            lanes = slice(i * 128, (i + 1) * 128)
-            hi, mid, low = split3(ga[lanes, :].T)
-            for k, term in enumerate((low, mid, hi)):
-                acat[:, k * pairs + i * 128 : k * pairs + (i + 1) * 128] = term
-
-    with jax.named_scope("agwait"):
-        await_all(x_all.at[slot(opp, core), :, part_a], ag_r.at[6])
-        cross(slot(opp, core), part_a)
-        await_all(x_all.at[slot(opp, core), :, part_b], ag_r.at[7])
-        cross(slot(opp, core), part_b)
-        await_all(x_all.at[pl.ds(other * chips, chips)], cross_r)
-
-    with jax.named_scope("wwait"):
-        weights[0].wait()
-        weights[1].wait()
-
-    with jax.named_scope("gateup"):
-        x_rows = x_all[...].reshape(rows, dim)
-
-        def gather(e):
-            xg[(e // 2) % 2] = dot(p_all[e * cap : (e + 2) * cap, :], x_rows).astype(BF16)
-
-        gather(0)
-        for e in range(n_exp):
-            if e % 2 == 0 and e + 2 < n_exp:
-                gather(e + 2)
-            xe = xg[(e // 2) % 2, (e % 2) * cap : (e % 2 + 1) * cap, :]
-            h_gate = dot(xe, wg[e])
-            h_up = dot(xe, wu[e])
-            hbuf[e * cap : (e + 1) * cap, :] = (jax.nn.silu(h_gate) * h_up).astype(BF16)
-
-    with jax.named_scope("dwait"):
-        weights[2].wait()
+        for i in range(pairs // 128):
+            e_one, e_two = i * 128 // cap, (i * 128 + 127) // cap
+            row_no = lax.broadcasted_iota(jnp.int32, (128, rows), 0) + i * 128
+            first = row_no < e_two * cap
+            pos = (row_no - jnp.where(first, e_one * cap, e_two * cap)).astype(F32)
+            hit = pos == jnp.where(first, place[e_one : e_one + 1, :], place[e_two : e_two + 1, :])
+            gated = jnp.where(hit, jnp.where(first, gmat[e_one : e_one + 1, :], gmat[e_two : e_two + 1, :]), 0.0)
+            p_all[i * 128 : (i + 1) * 128, :] = jnp.where(hit, 1.0, 0.0).astype(BF16)
+            for k, term in enumerate(reversed(split3(gated.T))):
+                for b in range(ep_size):
+                    to_row = ((b % CORES) * chips + b // CORES) * tok
+                    acat[to_row : to_row + tok, k * pairs + i * 128 : k * pairs + (i + 1) * 128] = term[b * tok : (b + 1) * tok, :]
+
+    n_near = rows - CORES * tok
+    stack = pairs // 4
+
+    def gather_near(k):
+        at = slice(k * stack, (k + 1) * stack)
+        xg[at, :] = dot(p_all[at, 0:n_near], x_all[0 : ep_size - CORES].reshape(n_near, dim)).astype(BF16)
+
+    with jax.named_scope("nearrest"):
+        near_rest()
+    with jax.named_scope("nearwait"):
+        await_all(x_all.at[0 : chips - 1], cross_r.at[0])
+    with jax.named_scope("near0"):
+        gather_near(0)
+    with jax.named_scope("far"):
+        await_all(x_all.at[mine, :, part_a], ag_r.at[6])
+        cross(opp, part_a, cross_r.at[1])
+        await_all(x_all.at[mine, :, part_b], ag_r.at[7])
+        cross(opp, part_b, cross_r.at[1])
+    with jax.named_scope("near1"):
+        for k in range(1, 4):
+            gather_near(k)
+    with jax.named_scope("farwait"):
+        await_all(x_all.at[mine], cross_r.at[1])
+        for copy in weights[:3]:
+            copy.wait()
 
     part = []
 
@@ -223,17 +231,17 @@
     def send(j):
         part[j].wait_recv()
         tbuf[j] = (sbuf[j, core] + d2d[j]).reshape(chips, tok, COLS)
-        remote(tbuf.at[j, opp, :, lo], hop.at[j, :, lo], dev(right, core), hop_s, hop_r.at[j])
-        remote(tbuf.at[j, opp, :, up], hop.at[j, :, up], dev(left, core), hop_s, hop_r.at[j])
+        remote(tbuf.at[j, POS_FAR, :, lo], hop.at[j, :, lo], dev(right, core), hop_s, hop_r.at[j])
+        remote(tbuf.at[j, POS_FAR, :, up], hop.at[j, :, up], dev(left, core), hop_s, hop_r.at[j])
 
     def direct(j):
-        remote(tbuf.at[j, right, :, up], froml.at[j, :, up], dev(right, core), dir_s, end_r.at[0, j // half_blk])
-        remote(tbuf.at[j, left, :, lo], fromr.at[j, :, lo], dev(left, core), dir_s, end_r.at[1, j // half_blk])
+        remote(tbuf.at[j, POS_RIGHT, :, up], froml.at[j, :, up], dev(right, core), dir_s, end_r.at[0, j // half_blk])
+        remote(tbuf.at[j, POS_LEFT, :, lo], fromr.at[j, :, lo], dev(left, core), dir_s, end_r.at[1, j // half_blk])
 
     def relay(j):
         await_all(hop.at[j], hop_r.at[j])
-        rel[j, :, lo] = hop[j, :, lo] + tbuf[j, right, :, lo]
-        rel[j, :, up] = hop[j, :, up] + tbuf[j, left, :, up]
+        rel[j, :, lo] = hop[j, :, lo] + tbuf[j, POS_RIGHT, :, lo]
+        rel[j, :, up] = hop[j, :, up] + tbuf[j, POS_LEFT, :, up]
         remote(rel.at[j, :, lo], froml.at[j, :, lo], dev(right, core), rel_s, end_r.at[0, j // half_blk])
         remote(rel.at[j, :, up], fromr.at[j, :, up], dev(left, core), rel_s, end_r.at[1, j // half_blk])
 
@@ -243,25 +251,36 @@
         await_all(fromr.at[blks], end_r.at[1, k])
         for j in range(k * half_blk, (k + 1) * half_blk):
             cols = slice(j * COLS, (j + 1) * COLS)
-            routed = (tbuf[j, chip] + froml[j]) + fromr[j]
-            obuf[:, cols] = ((hid[:, cols].astype(F32) + shared[:, cols].astype(F32)) + routed).astype(BF16)
-        cols = slice(k * half_blk * COLS, (k + 1) * half_blk * COLS)
-        pltpu.make_async_copy(obuf.at[:, cols], out_ref.at[:, cols], o_sem).start()
+            routed = (tbuf[j, POS_OWN] + froml[j]) + fromr[j]
+            out_ref[:, cols] = ((hid[:, cols].astype(F32) + shared[:, cols].astype(F32)) + routed).astype(BF16)
 
     def scoped(f, j):
         with jax.named_scope(f"{f.__name__}{j}"):
             f(j)
 
-    last(0)
+    with jax.named_scope("gateup"):
+        x_far = x_all[ep_size - CORES : ep_size].reshape(CORES * tok, dim)
+        for e in range(n_exp):
+            if e % 2 == 0:
+                two = slice(e * cap, (e + 2) * cap)
+                xg[two, :] = xg[two, :] + dot(p_all[two, n_near:], x_far).astype(BF16)
+            own = slice(e * cap, (e + 1) * cap)
+            h_gate = dot(xg[own, :], wg[e])
+            h_up = dot(xg[own, :], wu[e])
+            hbuf[own, :] = (jax.nn.silu(h_gate) * h_up).astype(BF16)
+        last(0)
+        compute(0)
+    weights[3].wait()
     for j in range(n_blk):
-        scoped(compute, j)
+        if j:
+            scoped(compute, j)
         if j >= 1:
             scoped(send, j - 1)
             scoped(direct, j - 1)
     scoped(send, n_blk - 1)
 
     with jax.named_scope("shared"):
-        for copy in weights[3:]:
+        for copy in weights[4:]:
             copy.wait()
         xs = x_all[mine]
         mid_cols = hsh.shape[1] // 2
@@ -290,7 +309,12 @@
         await_all(hop, hop_s)
         await_all(froml, dir_s)
         await_all(rel, rel_s)
-        pltpu.make_async_copy(obuf, out_ref, o_sem).wait()
+
+
+def put_kernel(src, dst, o_sem):
+    copy = pltpu.make_async_copy(src, dst, o_sem)
+    copy.start()
+    copy.wait()
 
 
 def solution(mesh):
@@ -312,24 +336,25 @@
             vm(w_gate.shape, BF16), vm(w_up.shape, BF16), vm(w_down.shape, BF16),
             vm(ws_gate.shape, BF16), vm(ws_up.shape, BF16), vm(ws_down.shape, BF16),
             vm((ep_size, tok, dim), BF16), vm((ep_size, n_exp, 128), F32), vm((ep_size, n_exp, 128), F32),
-            vm((pairs, rows), BF16), vm((pairs, rows), F32),
+            vm((pairs, rows), BF16),
             vm((rows, 3 * pairs), BF16),
-            vm((2, 2 * cap, dim), BF16), vm((pairs, inter), BF16), vm((2, 3 * pairs, COLS), BF16),
+            vm((pairs, dim), BF16), vm((pairs, inter), BF16), vm((2, 3 * pairs, COLS), BF16),
             vm((n_blk, CORES, chips * tok, COLS), F32), vm((n_blk, chips * tok, COLS), F32), vm((n_blk, chips, tok, COLS), F32),
             vm((n_blk, tok, COLS), F32), vm((n_blk, tok, COLS), F32), vm((n_blk, tok, COLS), F32), vm((n_blk, tok, COLS), F32),
-            vm((tok, s_inter), BF16), vm((tok, dim), BF16), vm((tok, dim), BF16),
-            sem((4,)), sem((6,)), sem, sem, sem, sem, sem, sem, sem, sem,
-            sem((8,)), sem, sem, sem((n_blk,)), sem((n_blk,)), sem((2, 2)),
+            vm((tok, s_inter), BF16), vm((tok, dim), BF16),
+            sem((4,)), sem((7,)), sem, sem, sem, sem, sem, sem, sem,
+            sem((8,)), sem((2,)), sem, sem((n_blk,)), sem((n_blk,)), sem((2, 2)),
         ]
-        return pl.pallas_call(
+        result = pl.pallas_call(
             functools.partial(moe_kernel, ep_size, cap),
-            out_shape=jax.ShapeDtypeStruct((tok, dim), BF16),
+            out_shape=pltpu.VMEM((tok, dim), BF16),
             in_specs=[pl.BlockSpec(memory_space=pl.ANY)] * 10,
-            out_specs=pl.BlockSpec(memory_space=pl.ANY),
+            out_specs=pl.BlockSpec(memory_space=pltpu.VMEM),
             scratch_shapes=scratch,
-            compiler_params=pltpu.CompilerParams(collective_id=0, has_side_effects=True, vmem_limit_bytes=67_000_000),
+            compiler_params=pltpu.CompilerParams(collective_id=0, has_side_effects=True, vmem_limit_bytes=64_900_000),
             name="moe_block",
         )(hidden_in, norm_gain.reshape(dim // 128, 128), router_w, w_gate, w_up, w_down, ws_gate, ws_up, ws_down, expert_ids.T)
+        return result
 
     row_spec = P(("dp", "ep"), None)
     in_specs = (row_spec, P(), P(), P("ep"), P("ep"), P("ep"), P(), P(), P(), row_spec)

time: 35.7 us -> 34.1 us (0.955)
  local copies, waits for them, and re-layouts: 1.58 us -> 0.66 us
  Pallas kernels: 34 us -> 33.3 us
    unnamed x1, local copies, waits for them, and re-layouts: 1.58 us -> 0.66 us
    pallas_call x1, Pallas kernels: 34 us -> 33.3 us  [local_block(): pl.pallas_call(functools.partial(moe_kernel, ep_size, cap), out_shape=plt...]
where the time goes in v3:
time: 34.1 us; the launch traced here: 34 us
  Pallas kernels  33.3 us (98%)
  local copies, waits for them, and re-layouts  0.66 us (2%)
    pallas_call x1, Pallas kernels, local_block(): pl.pallas_call(functools.partial(moe_kernel, ep_size, cap), out_shape=plt...  33.3 us

profile of v3, /device:TPU:112, one launch (start us, length us, event | category | flops | bytes accessed | tf_op | source)
XLA Modules:
  0.0 34.0 jit_solution(15291515614635174888)
XLA Ops:
  0.0 33.3 %moe_block.1 = bf16[48,1536]{1,0:T(8,128)(2,1)S(1)} custom-call(bf16[48,1536]{1,0:T(8,128)(2,1)} %hid_h.1, f32[12,128]{1,0:T(8,128)} %bitcast.2, f32[64,1536]{1,0:T(8,128)} %rw_h.1, bf16[8,1536,512]{2,1,0:T(8,128)(2,1)} %wg_h.1, bf16[8,1536,512]{2,1,0:T(8,128)(2,1)} %wu_h.1, bf16[8,512,1536]{2,1,0:T(8,128)(2,1)} %wd_h.1, bf16[1536,1024]{1,0:T(8,128)(2,1)} %sg_h.1, ...), custom_call_target="tpu_custom_call" | custom-call | tf_op jit(solution)/shard_map/moe_block/pallas_call | solution.py:348
  33.3 0.7 %copy.12 = bf16[48,1536]{1,0:T(8,128)(2,1)} copy(bf16[48,1536]{1,0:T(8,128)(2,1)S(1)} %moe_block.1) | data formatting | bytes 294912

commit v4 on v3

--- a/solution.py
+++ b/solution.py
@@ -12,6 +12,7 @@
 GROUPS = 8
 GROUP_LIMIT = 4
 CORES = 2
+S_ROW = (0, 1, 2, 4, 5, 6, 3, 7)
 POS_OWN, POS_RIGHT, POS_LEFT, POS_FAR = range(4)
 COLS = 256
 MESH = pl.DeviceIdType.MESH
@@ -55,9 +56,12 @@
     other = 1 - core
     right, left, opp = (chip + 1) % chips, (chip + chips - 1) % chips, (chip + 2) % chips
 
-    def slot(a_chip, a_core, at=None):
-        away = (a_chip - (chip if at is None else at) + chips) % chips
-        return (away + away // 2 - 2 * (away // 3)) * CORES + a_core
+    def slot(a_chip, a_core, at_chip=chip, at_core=core):
+        away = (a_chip - at_chip + chips) % chips
+        pos = away + away // 2 - 2 * (away // 3)
+        cross_core = (a_core + at_core) % CORES
+        is_far = pos // POS_FAR
+        return pos + (chips - 1) * cross_core + is_far * (chips - 1 - (chips - 2) * cross_core)
 
     def dev(a_chip, a_core):
         return {"ep": a_chip * CORES + a_core}
@@ -84,7 +88,6 @@
     for k in range(1, ep_size):
         pl.semaphore_signal(barrier, inc=1, device_id={"ep": (me + k) % ep_size}, device_id_type=MESH)
 
-    mine = slot(chip, core)
     with jax.named_scope("norm"):
         ins[0].wait()
         ins[1].wait()
@@ -92,7 +95,7 @@
         inv_rms = lax.rsqrt(jnp.mean(x_f32 * x_f32, axis=-1, keepdims=True) + NORM_EPS)
         gain_row = jnp.concatenate([gain[i : i + 1, :] for i in range(dim // 128)], axis=1)
         x_norm = (x_f32 * inv_rms * gain_row).astype(BF16)
-        x_all[mine] = x_norm
+        x_all[0] = x_norm
 
     with jax.named_scope("barwait"):
         pl.semaphore_wait(barrier, ep_size - 1)
@@ -102,12 +105,12 @@
     part_a, part_b = slice(0, half), slice(half, dim)
 
     def spread(a_chip, cols, to, r_sem):
-        src, dst = x_all.at[slot(a_chip, core), :, cols], x_all.at[slot(a_chip, core, to), :, cols]
+        src, dst = x_all.at[slot(a_chip, core), :, cols], x_all.at[slot(a_chip, core, to, core), :, cols]
         return remote(src, dst, dev(to, core), ring_s, r_sem)
 
     def cross(a_chip, cols, r_sem):
-        ref = x_all.at[slot(a_chip, core), :, cols]
-        remote(ref, ref, dev(chip, other), cross_s, r_sem)
+        src, dst = x_all.at[slot(a_chip, core), :, cols], x_all.at[slot(a_chip, core, chip, other), :, cols]
+        remote(src, dst, dev(chip, other), cross_s, r_sem)
 
     ra, lb = [], []
     for k in range(2):
@@ -129,10 +132,10 @@
         gt_send[...] = jnp.full(gt_send.shape, -1.0, F32)
         for d in range(ep_size):
             gt_send[d, :, 0:tok] = gates[d * n_exp : (d + 1) * n_exp, :]
-        gt_all[mine] = gt_send[me]
+        gt_all[0] = gt_send[me]
         for k in range(1, ep_size):
             to = (me + k) % ep_size
-            remote(gt_send.at[to], gt_all.at[slot(chip, core, to // CORES)], {"ep": to}, tile_s, tile_r)
+            remote(gt_send.at[to], gt_all.at[slot(chip, core, to // CORES, to % CORES)], {"ep": to}, tile_s, tile_r)
 
     rb = spread(chip, part_b, right, ag_r.at[4])
     la = spread(chip, part_a, left, ag_r.at[5])
@@ -142,16 +145,16 @@
         for k in range(2):
             ra[k].wait_recv()
             spread(left, q[k], right, ag_r.at[6])
-            cross(left, q[k], cross_r.at[0])
+            cross(left, q[k], cross_r.at[1])
             lb[k].wait_recv()
             spread(right, q[2 + k], left, ag_r.at[7])
-            cross(right, q[2 + k], cross_r.at[0])
+            cross(right, q[2 + k], cross_r.at[1])
 
     def near_rest():
         rb.wait_recv()
-        cross(left, part_b, cross_r.at[0])
+        cross(left, part_b, cross_r.at[1])
         la.wait_recv()
-        cross(right, part_a, cross_r.at[0])
+        cross(right, part_a, cross_r.at[1])
 
     with jax.named_scope("tilewait"):
         await_all(gt_all.at[0 : ep_size - 1], tile_r)
@@ -178,32 +181,23 @@
             p_all[i * 128 : (i + 1) * 128, :] = jnp.where(hit, 1.0, 0.0).astype(BF16)
             for k, term in enumerate(reversed(split3(gated.T))):
                 for b in range(ep_size):
-                    to_row = ((b % CORES) * chips + b // CORES) * tok
+                    to_row = S_ROW[b] * tok
                     acat[to_row : to_row + tok, k * pairs + i * 128 : k * pairs + (i + 1) * 128] = term[b * tok : (b + 1) * tok, :]
 
-    n_near = rows - CORES * tok
-    stack = pairs // 4
-
-    def gather_near(k):
-        at = slice(k * stack, (k + 1) * stack)
-        xg[at, :] = dot(p_all[at, 0:n_near], x_all[0 : ep_size - CORES].reshape(n_near, dim)).astype(BF16)
-
+    n_near = rows // 2
     with jax.named_scope("nearrest"):
         near_rest()
     with jax.named_scope("nearwait"):
-        await_all(x_all.at[0 : chips - 1], cross_r.at[0])
-    with jax.named_scope("near0"):
-        gather_near(0)
+        await_all(x_all.at[0], cross_r.at[0])
+    with jax.named_scope("near"):
+        xg[...] = dot(p_all[:, 0:n_near], x_all[0 : ep_size // 2].reshape(n_near, dim)).astype(BF16)
     with jax.named_scope("far"):
-        await_all(x_all.at[mine, :, part_a], ag_r.at[6])
+        await_all(x_all.at[0, :, part_a], ag_r.at[6])
         cross(opp, part_a, cross_r.at[1])
-        await_all(x_all.at[mine, :, part_b], ag_r.at[7])
+        await_all(x_all.at[0, :, part_b], ag_r.at[7])
         cross(opp, part_b, cross_r.at[1])
-    with jax.named_scope("near1"):
-        for k in range(1, 4):
-            gather_near(k)
     with jax.named_scope("farwait"):
-        await_all(x_all.at[mine], cross_r.at[1])
+        await_all(x_all.at[0 : chips - 1], cross_r.at[1])
         for copy in weights[:3]:
             copy.wait()
 
@@ -223,14 +217,14 @@
             last(j + 1)
         for k in range(CORES):
             sbuf[j, k] = dot(acat[k * chips * tok : (k + 1) * chips * tok, :], ybuf[j % 2])
-        part.append(remote(sbuf.at[j, other], d2d.at[j], dev(chip, other), d2d_s, d2d_r.at[j]))
+        part.append(remote(sbuf.at[j, 1], d2d.at[j], dev(chip, other), d2d_s, d2d_r.at[j]))
 
     lo, up = slice(0, hc), slice(hc, COLS)
     half_blk = n_blk // 2
 
     def send(j):
         part[j].wait_recv()
-        tbuf[j] = (sbuf[j, core] + d2d[j]).reshape(chips, tok, COLS)
+        tbuf[j] = (sbuf[j, 0] + d2d[j]).reshape(chips, tok, COLS)
         remote(tbuf.at[j, POS_FAR, :, lo], hop.at[j, :, lo], dev(right, core), hop_s, hop_r.at[j])
         remote(tbuf.at[j, POS_FAR, :, up], hop.at[j, :, up], dev(left, core), hop_s, hop_r.at[j])
 
@@ -259,7 +253,7 @@
             f(j)
 
     with jax.named_scope("gateup"):
-        x_far = x_all[ep_size - CORES : ep_size].reshape(CORES * tok, dim)
+        x_far = x_all[ep_size // 2 : ep_size].reshape(rows - n_near, dim)
         for e in range(n_exp):
             if e % 2 == 0:
                 two = slice(e * cap, (e + 2) * cap)
@@ -282,7 +276,7 @@
     with jax.named_scope("shared"):
         for copy in weights[4:]:
             copy.wait()
-        xs = x_all[mine]
+        xs = x_all[0]
         mid_cols = hsh.shape[1] // 2
 
         def shared_part(k):

time: 34.1 us -> 33.3 us (0.977)
  Pallas kernels: 33.3 us -> 32.5 us
    pallas_call x1, Pallas kernels: 33.3 us -> 32.5 us  [local_block(): pl.pallas_call(functools.partial(moe_kernel, ep_size, cap), out_shape=plt...]
where the time goes in v4:
time: 33.3 us; the launch traced here: 33.2 us
  Pallas kernels  32.5 us (98%)
  local copies, waits for them, and re-layouts  0.66 us (2%)
    pallas_call x1, Pallas kernels, local_block(): pl.pallas_call(functools.partial(moe_kernel, ep_size, cap), out_shape=plt...  32.5 us

profile of v4, /device:TPU:112, one launch (start us, length us, event | category | flops | bytes accessed | tf_op | source)
XLA Modules:
  0.0 33.2 jit_solution(17161801012851946202)
XLA Ops:
  0.0 32.5 %moe_block.1 = bf16[48,1536]{1,0:T(8,128)(2,1)S(1)} custom-call(bf16[48,1536]{1,0:T(8,128)(2,1)} %hid_h.1, f32[12,128]{1,0:T(8,128)} %bitcast.2, f32[64,1536]{1,0:T(8,128)} %rw_h.1, bf16[8,1536,512]{2,1,0:T(8,128)(2,1)} %wg_h.1, bf16[8,1536,512]{2,1,0:T(8,128)(2,1)} %wu_h.1, bf16[8,512,1536]{2,1,0:T(8,128)(2,1)} %wd_h.1, bf16[1536,1024]{1,0:T(8,128)(2,1)} %sg_h.1, ...), custom_call_target="tpu_custom_call" | custom-call | tf_op jit(solution)/shard_map/moe_block/pallas_call | solution.py:342
  32.5 0.7 %copy.12 = bf16[48,1536]{1,0:T(8,128)(2,1)} copy(bf16[48,1536]{1,0:T(8,128)(2,1)S(1)} %moe_block.1) | data formatting | bytes 294912

commit v5 on v4

--- a/solution.py
+++ b/solution.py
@@ -15,6 +15,7 @@
 S_ROW = (0, 1, 2, 4, 5, 6, 3, 7)
 POS_OWN, POS_RIGHT, POS_LEFT, POS_FAR = range(4)
 COLS = 256
+CHUNK = 512
 MESH = pl.DeviceIdType.MESH
 F32 = jnp.float32
 BF16 = jnp.bfloat16
@@ -78,7 +79,9 @@
     for copy in ins:
         copy.start()
     early, late = slice(0, COLS), slice(COLS, dim)
-    fetches = ((wg_h, wg), (wu_h, wu), (wd_h.at[:, :, early], wd.at[:, :, early]), (wd_h.at[:, :, late], wd.at[:, :, late]), (sg_h, sg), (su_h, su), (sd_h, sd))
+    chunk = (slice(0, CHUNK), slice(CHUNK, dim))
+    fetches = [(h.at[:, rng, :], v.at[:, rng, :]) for rng in chunk for h, v in ((wg_h, wg), (wu_h, wu))]
+    fetches += [(wd_h.at[:, :, early], wd.at[:, :, early]), (wd_h.at[:, :, late], wd.at[:, :, late]), (sg_h, sg), (su_h, su), (sd_h, sd)]
     weights = []
     for i, (s, d) in enumerate(fetches):
         weights.append(pltpu.make_async_copy(s, d, w_sem.at[i]))
@@ -100,9 +103,8 @@
     with jax.named_scope("barwait"):
         pl.semaphore_wait(barrier, ep_size - 1)
 
-    half = dim // 2
-    q = [slice(k * half // 2, (k + 1) * half // 2) for k in range(4)]
-    part_a, part_b = slice(0, half), slice(half, dim)
+    side_a = [slice(0, CHUNK // 2), slice(CHUNK, (CHUNK + dim) // 2)]
+    side_b = [slice(CHUNK // 2, CHUNK), slice((CHUNK + dim) // 2, dim)]
 
     def spread(a_chip, cols, to, r_sem):
         src, dst = x_all.at[slot(a_chip, core), :, cols], x_all.at[slot(a_chip, core, to, core), :, cols]
@@ -114,8 +116,8 @@
 
     ra, lb = [], []
     for k in range(2):
-        ra.append(spread(chip, q[k], right, ag_r.at[k]))
-        lb.append(spread(chip, q[2 + k], left, ag_r.at[2 + k]))
+        ra.append(spread(chip, side_a[k], right, ag_r.at[k]))
+        lb.append(spread(chip, side_b[k], left, ag_r.at[2 + k]))
 
     with jax.named_scope("router"):
         ins[2].wait()
@@ -137,24 +139,26 @@
             to = (me + k) % ep_size
             remote(gt_send.at[to], gt_all.at[slot(chip, core, to // CORES, to % CORES)], {"ep": to}, tile_s, tile_r)
 
-    rb = spread(chip, part_b, right, ag_r.at[4])
-    la = spread(chip, part_a, left, ag_r.at[5])
+    for k in range(2):
+        spread(chip, side_b[k], right, ag_r.at[4])
+        spread(chip, side_a[k], left, ag_r.at[5])
     cross(chip, slice(0, dim), cross_r.at[0])
 
     with jax.named_scope("relays"):
         for k in range(2):
             ra[k].wait_recv()
-            spread(left, q[k], right, ag_r.at[6])
-            cross(left, q[k], cross_r.at[1])
+            spread(left, side_a[k], right, ag_r.at[6 + 2 * k])
+            cross(left, side_a[k], cross_r.at[1])
             lb[k].wait_recv()
-            spread(right, q[2 + k], left, ag_r.at[7])
-            cross(right, q[2 + k], cross_r.at[1])
+            spread(right, side_b[k], left, ag_r.at[7 + 2 * k])
+            cross(right, side_b[k], cross_r.at[1])
 
     def near_rest():
-        rb.wait_recv()
-        cross(left, part_b, cross_r.at[1])
-        la.wait_recv()
-        cross(right, part_a, cross_r.at[1])
+        await_all(x_all.at[0, :, 0 : dim // 2], ag_r.at[4])
+        await_all(x_all.at[0, :, 0 : dim // 2], ag_r.at[5])
+        for k in range(2):
+            cross(left, side_b[k], cross_r.at[1])
+            cross(right, side_a[k], cross_r.at[1])
 
     with jax.named_scope("tilewait"):
         await_all(gt_all.at[0 : ep_size - 1], tile_r)
@@ -189,16 +193,59 @@
         near_rest()
     with jax.named_scope("nearwait"):
         await_all(x_all.at[0], cross_r.at[0])
-    with jax.named_scope("near"):
-        xg[...] = dot(p_all[:, 0:n_near], x_all[0 : ep_size // 2].reshape(n_near, dim)).astype(BF16)
-    with jax.named_scope("far"):
-        await_all(x_all.at[0, :, part_a], ag_r.at[6])
-        cross(opp, part_a, cross_r.at[1])
-        await_all(x_all.at[0, :, part_b], ag_r.at[7])
-        cross(opp, part_b, cross_r.at[1])
-    with jax.named_scope("farwait"):
-        await_all(x_all.at[0 : chips - 1], cross_r.at[1])
-        for copy in weights[:3]:
+    x_near = x_all.at[0 : ep_size // 2]
+    x_rest = x_all.at[ep_size // 2 : ep_size]
+
+    def gather_near(k):
+        with jax.named_scope(f"near{k}"):
+            xg[:, chunk[k]] = dot(p_all[:, 0:n_near], x_near[:, :, chunk[k]].reshape(n_near, -1)).astype(BF16)
+
+    def pass_far(k):
+        with jax.named_scope(f"far{k}"):
+            await_all(x_all.at[0, :, side_a[k]], ag_r.at[6 + 2 * k])
+            await_all(x_all.at[0, :, side_b[k]], ag_r.at[7 + 2 * k])
+            cross(opp, chunk[k], cross_r.at[2 + k])
+
+    def gate_up(k):
+        def gather_far(p):
+            two = slice(2 * p * cap, 2 * (p + 1) * cap)
+            xg[two, chunk[k]] = xg[two, chunk[k]] + dot(p_all[two, n_near:], x_rest[:, :, chunk[k]].reshape(rows - n_near, -1)).astype(BF16)
+
+        gather_far(0)
+        for e in range(n_exp):
+            if e % 2 == 0 and e + 2 < n_exp:
+                gather_far(e // 2 + 1)
+            own = slice(e * cap, (e + 1) * cap)
+            row = e % 4 * cap
+            xe = xg[own, chunk[k]]
+            h = []
+            for m, w in enumerate((wg, wu)):
+                total_h = dot(xe, w[e, chunk[k], :])
+                for c in range(2):
+                    spot = sbuf.at[4 * m + 2 * c + e // 4, row // (chips * tok), row % (chips * tok) : row % (chips * tok) + cap, :]
+                    piece = total_h[:, c * COLS : (c + 1) * COLS]
+                    if k == 0:
+                        spot[...] = piece
+                    else:
+                        h.append(spot[...] + piece)
+            if k:
+                for c in range(2):
+                    hbuf[own, c * COLS : (c + 1) * COLS] = (jax.nn.silu(h[c]) * h[2 + c]).astype(BF16)
+
+    gather_near(0)
+    pass_far(0)
+    gather_near(1)
+    pass_far(1)
+    with jax.named_scope("farwait0"):
+        await_all(x_all.at[0 : chips - 2], cross_r.at[1])
+        await_all(x_all.at[0, :, chunk[0]], cross_r.at[2])
+        weights[0].wait()
+        weights[1].wait()
+    with jax.named_scope("gateup0"):
+        gate_up(0)
+    with jax.named_scope("farwait1"):
+        await_all(x_all.at[0, :, chunk[1]], cross_r.at[3])
+        for copy in weights[2:5]:
             copy.wait()
 
     part = []
@@ -252,19 +299,11 @@
         with jax.named_scope(f"{f.__name__}{j}"):
             f(j)
 
-    with jax.named_scope("gateup"):
-        x_far = x_all[ep_size // 2 : ep_size].reshape(rows - n_near, dim)
-        for e in range(n_exp):
-            if e % 2 == 0:
-                two = slice(e * cap, (e + 2) * cap)
-                xg[two, :] = xg[two, :] + dot(p_all[two, n_near:], x_far).astype(BF16)
-            own = slice(e * cap, (e + 1) * cap)
-            h_gate = dot(xg[own, :], wg[e])
-            h_up = dot(xg[own, :], wu[e])
-            hbuf[own, :] = (jax.nn.silu(h_gate) * h_up).astype(BF16)
+    with jax.named_scope("gateup1"):
+        gate_up(1)
         last(0)
         compute(0)
-    weights[3].wait()
+    weights[5].wait()
     for j in range(n_blk):
         if j:
             scoped(compute, j)
@@ -274,7 +313,7 @@
     scoped(send, n_blk - 1)
 
     with jax.named_scope("shared"):
-        for copy in weights[4:]:
+        for copy in weights[6:]:
             copy.wait()
         xs = x_all[0]
         mid_cols = hsh.shape[1] // 2
@@ -333,11 +372,11 @@
             vm((pairs, rows), BF16),
             vm((rows, 3 * pairs), BF16),
             vm((pairs, dim), BF16), vm((pairs, inter), BF16), vm((2, 3 * pairs, COLS), BF16),
-            vm((n_blk, CORES, chips * tok, COLS), F32), vm((n_blk, chips * tok, COLS), F32), vm((n_blk, chips, tok, COLS), F32),
+            vm((8, CORES, chips * tok, COLS), F32), vm((n_blk, chips * tok, COLS), F32), vm((n_blk, chips, tok, COLS), F32),
             vm((n_blk, tok, COLS), F32), vm((n_blk, tok, COLS), F32), vm((n_blk, tok, COLS), F32), vm((n_blk, tok, COLS), F32),
             vm((tok, s_inter), BF16), vm((tok, dim), BF16),
-            sem((4,)), sem((7,)), sem, sem, sem, sem, sem, sem, sem,
-            sem((8,)), sem((2,)), sem, sem((n_blk,)), sem((n_blk,)), sem((2, 2)),
+            sem((4,)), sem((9,)), sem, sem, sem, sem, sem, sem, sem,
+            sem((10,)), sem((4,)), sem, sem((n_blk,)), sem((n_blk,)), sem((2, 2)),
         ]
         result = pl.pallas_call(
             functools.partial(moe_kernel, ep_size, cap),
@@ -345,7 +384,7 @@
             in_specs=[pl.BlockSpec(memory_space=pl.ANY)] * 10,
             out_specs=pl.BlockSpec(memory_space=pltpu.VMEM),
             scratch_shapes=scratch,
-            compiler_params=pltpu.CompilerParams(collective_id=0, has_side_effects=True, vmem_limit_bytes=64_900_000),
+            compiler_params=pltpu.CompilerParams(collective_id=0, has_side_effects=True, vmem_limit_bytes=65_800_000),
             name="moe_block",
         )(hidden_in, norm_gain.reshape(dim // 128, 128), router_w, w_gate, w_up, w_down, ws_gate, ws_up, ws_down, expert_ids.T)
         return result

time: 33.3 us -> 33.2 us (level)
  no operation moved by 1% of the time
where the time goes in v5:
time: 33.2 us; the launch traced here: 33.1 us
  Pallas kernels  32.4 us (98%)
  local copies, waits for them, and re-layouts  0.66 us (2%)
    pallas_call x1, Pallas kernels, local_block(): pl.pallas_call(functools.partial(moe_kernel, ep_size, cap), out_shape=plt...  32.4 us

profile of v5, /device:TPU:112, one launch (start us, length us, event | category | flops | bytes accessed | tf_op | source)
XLA Modules:
  0.0 33.1 jit_solution(11349107182225881597)
XLA Ops:
  0.0 32.4 %moe_block.1 = bf16[48,1536]{1,0:T(8,128)(2,1)S(1)} custom-call(bf16[48,1536]{1,0:T(8,128)(2,1)} %hid_h.1, f32[12,128]{1,0:T(8,128)} %bitcast.2, f32[64,1536]{1,0:T(8,128)} %rw_h.1, bf16[8,1536,512]{2,1,0:T(8,128)(2,1)} %wg_h.1, bf16[8,1536,512]{2,1,0:T(8,128)(2,1)} %wu_h.1, bf16[8,512,1536]{2,1,0:T(8,128)(2,1)} %wd_h.1, bf16[1536,1024]{1,0:T(8,128)(2,1)} %sg_h.1, ...), custom_call_target="tpu_custom_call" | custom-call | tf_op jit(solution)/shard_map/moe_block/pallas_call | solution.py:381
  32.4 0.7 %copy.12 = bf16[48,1536]{1,0:T(8,128)(2,1)} copy(bf16[48,1536]{1,0:T(8,128)(2,1)S(1)} %moe_block.1) | data formatting | bytes 294912

commit v6 on v5

--- a/solution.py
+++ b/solution.py
@@ -12,6 +12,7 @@
 GROUPS = 8
 GROUP_LIMIT = 4
 CORES = 2
+HUB = 1
 S_ROW = (0, 1, 2, 4, 5, 6, 3, 7)
 POS_OWN, POS_RIGHT, POS_LEFT, POS_FAR = range(4)
 COLS = 256
@@ -106,9 +107,9 @@
     side_a = [slice(0, CHUNK // 2), slice(CHUNK, (CHUNK + dim) // 2)]
     side_b = [slice(CHUNK // 2, CHUNK), slice((CHUNK + dim) // 2, dim)]
 
-    def spread(a_chip, cols, to, r_sem):
-        src, dst = x_all.at[slot(a_chip, core), :, cols], x_all.at[slot(a_chip, core, to, core), :, cols]
-        return remote(src, dst, dev(to, core), ring_s, r_sem)
+    def spread(a_chip, cols, to, r_sem, to_core=core):
+        src, dst = x_all.at[slot(a_chip, core), :, cols], x_all.at[slot(a_chip, core, to, to_core), :, cols]
+        return remote(src, dst, dev(to, to_core), ring_s, r_sem)
 
     def cross(a_chip, cols, r_sem):
         src, dst = x_all.at[slot(a_chip, core), :, cols], x_all.at[slot(a_chip, core, chip, other), :, cols]
@@ -147,10 +148,10 @@
     with jax.named_scope("relays"):
         for k in range(2):
             ra[k].wait_recv()
-            spread(left, side_a[k], right, ag_r.at[6 + 2 * k])
+            spread(left, side_a[k], right, ag_r.at[6 + 2 * k], HUB)
             cross(left, side_a[k], cross_r.at[1])
             lb[k].wait_recv()
-            spread(right, side_b[k], left, ag_r.at[7 + 2 * k])
+            spread(right, side_b[k], left, ag_r.at[7 + 2 * k], HUB)
             cross(right, side_b[k], cross_r.at[1])
 
     def near_rest():
@@ -196,15 +197,26 @@
     x_near = x_all.at[0 : ep_size // 2]
     x_rest = x_all.at[ep_size // 2 : ep_size]
 
+    far_slots = slice(ep_size - CORES, ep_size)
+
+    def far_wait(k):
+        @pl.when(core != HUB)
+        def _():
+            await_all(x_all.at[far_slots, :, chunk[k]], cross_r.at[2 + k])
+
     def gather_near(k):
         with jax.named_scope(f"near{k}"):
             xg[:, chunk[k]] = dot(p_all[:, 0:n_near], x_near[:, :, chunk[k]].reshape(n_near, -1)).astype(BF16)
 
     def pass_far(k):
         with jax.named_scope(f"far{k}"):
-            await_all(x_all.at[0, :, side_a[k]], ag_r.at[6 + 2 * k])
-            await_all(x_all.at[0, :, side_b[k]], ag_r.at[7 + 2 * k])
-            cross(opp, chunk[k], cross_r.at[2 + k])
+            @pl.when(core == HUB)
+            def _():
+                for r_sem, cols in ((6 + 2 * k, side_a[k]), (7 + 2 * k, side_b[k])):
+                    await_all(x_all.at[far_slots, :, cols], ag_r.at[r_sem])
+                for i in range(CORES):
+                    src, dst = x_all.at[ep_size - 1 - i, :, chunk[k]], x_all.at[ep_size - CORES + i, :, chunk[k]]
+                    remote(src, dst, dev(chip, other), cross_s, cross_r.at[2 + k])
 
     def gate_up(k):
         def gather_far(p):
@@ -238,13 +250,13 @@
     pass_far(1)
     with jax.named_scope("farwait0"):
         await_all(x_all.at[0 : chips - 2], cross_r.at[1])
-        await_all(x_all.at[0, :, chunk[0]], cross_r.at[2])
+        far_wait(0)
         weights[0].wait()
         weights[1].wait()
     with jax.named_scope("gateup0"):
         gate_up(0)
     with jax.named_scope("farwait1"):
-        await_all(x_all.at[0, :, chunk[1]], cross_r.at[3])
+        far_wait(1)
         for copy in weights[2:5]:
             copy.wait()
 
@@ -336,7 +348,14 @@
         scoped(finish, k)
     with jax.named_scope("drain"):
         await_all(x_all.at[0:3], ring_s)
-        await_all(x_all.at[0:chips], cross_s)
+        @pl.when(core == HUB)
+        def _():
+            await_all(x_all.at[0 : chips + 1], cross_s)
+
+        @pl.when(core != HUB)
+        def _():
+            await_all(x_all.at[0 : chips - 1], cross_s)
+
         await_all(gt_send.at[0 : ep_size - 1], tile_s)
         await_all(d2d, d2d_s)
         await_all(hop, hop_s)

time: 33.2 us -> 33 us (level)
    pallas_call x1, Pallas kernels: 32.4 us -> 32.1 us  [local_block(): pl.pallas_call(functools.partial(moe_kernel, ep_size, cap), out_shape=plt...]
where the time goes in v6:
time: 33 us; the launch traced here: 32.7 us
  Pallas kernels  32.1 us (97%)
  local copies, waits for them, and re-layouts  0.66 us (2%)
    pallas_call x1, Pallas kernels, local_block(): pl.pallas_call(functools.partial(moe_kernel, ep_size, cap), out_shape=plt...  32.1 us
    unnamed x1, local copies, waits for them, and re-layouts  0.66 us

profile of v6, /device:TPU:112, one launch (start us, length us, event | category | flops | bytes accessed | tf_op | source)
XLA Modules:
  0.0 32.7 jit_solution(893716586830562825)
XLA Ops:
  0.0 32.1 %moe_block.1 = bf16[48,1536]{1,0:T(8,128)(2,1)S(1)} custom-call(bf16[48,1536]{1,0:T(8,128)(2,1)} %hid_h.1, f32[12,128]{1,0:T(8,128)} %bitcast.2, f32[64,1536]{1,0:T(8,128)} %rw_h.1, bf16[8,1536,512]{2,1,0:T(8,128)(2,1)} %wg_h.1, bf16[8,1536,512]{2,1,0:T(8,128)(2,1)} %wu_h.1, bf16[8,512,1536]{2,1,0:T(8,128)(2,1)} %wd_h.1, bf16[1536,1024]{1,0:T(8,128)(2,1)} %sg_h.1, ...), custom_call_target="tpu_custom_call" | custom-call | tf_op jit(solution)/shard_map/moe_block/pallas_call | solution.py:400
  32.1 0.7 %copy.12 = bf16[48,1536]{1,0:T(8,128)(2,1)} copy(bf16[48,1536]{1,0:T(8,128)(2,1)S(1)} %moe_block.1) | data formatting | bytes 294912

commit v7 on v6

--- a/solution.py
+++ b/solution.py
@@ -141,25 +141,24 @@
             remote(gt_send.at[to], gt_all.at[slot(chip, core, to // CORES, to % CORES)], {"ep": to}, tile_s, tile_r)
 
     for k in range(2):
-        spread(chip, side_b[k], right, ag_r.at[4])
-        spread(chip, side_a[k], left, ag_r.at[5])
+        spread(chip, side_b[k], right, ag_r.at[4 + k])
+        spread(chip, side_a[k], left, ag_r.at[4 + k])
     cross(chip, slice(0, dim), cross_r.at[0])
 
     with jax.named_scope("relays"):
         for k in range(2):
             ra[k].wait_recv()
             spread(left, side_a[k], right, ag_r.at[6 + 2 * k], HUB)
-            cross(left, side_a[k], cross_r.at[1])
+            cross(left, side_a[k], cross_r.at[1 + k])
             lb[k].wait_recv()
             spread(right, side_b[k], left, ag_r.at[7 + 2 * k], HUB)
-            cross(right, side_b[k], cross_r.at[1])
-
-    def near_rest():
-        await_all(x_all.at[0, :, 0 : dim // 2], ag_r.at[4])
-        await_all(x_all.at[0, :, 0 : dim // 2], ag_r.at[5])
-        for k in range(2):
-            cross(left, side_b[k], cross_r.at[1])
-            cross(right, side_a[k], cross_r.at[1])
+            cross(right, side_b[k], cross_r.at[1 + k])
+
+    def near_rest(k):
+        with jax.named_scope(f"rest{k}"):
+            await_all(x_all.at[0, :, chunk[k]], ag_r.at[4 + k])
+            cross(left, side_b[k], cross_r.at[1 + k])
+            cross(right, side_a[k], cross_r.at[1 + k])
 
     with jax.named_scope("tilewait"):
         await_all(gt_all.at[0 : ep_size - 1], tile_r)
@@ -190,8 +189,6 @@
                     acat[to_row : to_row + tok, k * pairs + i * 128 : k * pairs + (i + 1) * 128] = term[b * tok : (b + 1) * tok, :]
 
     n_near = rows // 2
-    with jax.named_scope("nearrest"):
-        near_rest()
     with jax.named_scope("nearwait"):
         await_all(x_all.at[0], cross_r.at[0])
     x_near = x_all.at[0 : ep_size // 2]
@@ -202,7 +199,7 @@
     def far_wait(k):
         @pl.when(core != HUB)
         def _():
-            await_all(x_all.at[far_slots, :, chunk[k]], cross_r.at[2 + k])
+            await_all(x_all.at[far_slots, :, chunk[k]], cross_r.at[3 + k])
 
     def gather_near(k):
         with jax.named_scope(f"near{k}"):
@@ -216,7 +213,7 @@
                     await_all(x_all.at[far_slots, :, cols], ag_r.at[r_sem])
                 for i in range(CORES):
                     src, dst = x_all.at[ep_size - 1 - i, :, chunk[k]], x_all.at[ep_size - CORES + i, :, chunk[k]]
-                    remote(src, dst, dev(chip, other), cross_s, cross_r.at[2 + k])
+                    remote(src, dst, dev(chip, other), cross_s, cross_r.at[3 + k])
 
     def gate_up(k):
         def gather_far(p):
@@ -244,18 +241,21 @@
                 for c in range(2):
                     hbuf[own, c * COLS : (c + 1) * COLS] = (jax.nn.silu(h[c]) * h[2 + c]).astype(BF16)
 
+    near_rest(0)
     gather_near(0)
+    near_rest(1)
     pass_far(0)
     gather_near(1)
     pass_far(1)
     with jax.named_scope("farwait0"):
-        await_all(x_all.at[0 : chips - 2], cross_r.at[1])
+        await_all(x_all.at[0 : chips - 2, :, chunk[0]], cross_r.at[1])
         far_wait(0)
         weights[0].wait()
         weights[1].wait()
     with jax.named_scope("gateup0"):
         gate_up(0)
     with jax.named_scope("farwait1"):
+        await_all(x_all.at[0 : chips - 2, :, chunk[1]], cross_r.at[2])
         far_wait(1)
         for copy in weights[2:5]:
             copy.wait()
@@ -395,7 +395,7 @@
             vm((n_blk, tok, COLS), F32), vm((n_blk, tok, COLS), F32), vm((n_blk, tok, COLS), F32), vm((n_blk, tok, COLS), F32),
             vm((tok, s_inter), BF16), vm((tok, dim), BF16),
             sem((4,)), sem((9,)), sem, sem, sem, sem, sem, sem, sem,
-            sem((10,)), sem((4,)), sem, sem((n_blk,)), sem((n_blk,)), sem((2, 2)),
+            sem((10,)), sem((5,)), sem, sem((n_blk,)), sem((n_blk,)), sem((2, 2)),
         ]
         result = pl.pallas_call(
             functools.partial(moe_kernel, ep_size, cap),

time: 33 us -> 32.8 us (level)
  no operation moved by 1% of the time
where the time goes in v7:
time: 32.8 us; the launch traced here: 32.6 us
  Pallas kernels  31.9 us (97%)
  local copies, waits for them, and re-layouts  0.66 us (2%)
    pallas_call x1, Pallas kernels, local_block(): pl.pallas_call(functools.partial(moe_kernel, ep_size, cap), out_shape=plt...  31.9 us
    unnamed x1, local copies, waits for them, and re-layouts  0.66 us

profile of v7, /device:TPU:112, one launch (start us, length us, event | category | flops | bytes accessed | tf_op | source)
XLA Modules:
  0.0 32.6 jit_solution(17169985781669818278)
XLA Ops:
  0.0 31.9 %moe_block.1 = bf16[48,1536]{1,0:T(8,128)(2,1)S(1)} custom-call(bf16[48,1536]{1,0:T(8,128)(2,1)} %hid_h.1, f32[12,128]{1,0:T(8,128)} %bitcast.2, f32[64,1536]{1,0:T(8,128)} %rw_h.1, bf16[8,1536,512]{2,1,0:T(8,128)(2,1)} %wg_h.1, bf16[8,1536,512]{2,1,0:T(8,128)(2,1)} %wu_h.1, bf16[8,512,1536]{2,1,0:T(8,128)(2,1)} %wd_h.1, bf16[1536,1024]{1,0:T(8,128)(2,1)} %sg_h.1, ...), custom_call_target="tpu_custom_call" | custom-call | tf_op jit(solution)/shard_map/moe_block/pallas_call | solution.py:400
  31.9 0.7 %copy.12 = bf16[48,1536]{1,0:T(8,128)(2,1)} copy(bf16[48,1536]{1,0:T(8,128)(2,1)S(1)} %moe_block.1) | data formatting | bytes 294912

commit v8 on v7

--- a/solution.py
+++ b/solution.py
@@ -13,6 +13,7 @@
 GROUP_LIMIT = 4
 CORES = 2
 HUB = 1
+SPLIT = 4
 S_ROW = (0, 1, 2, 4, 5, 6, 3, 7)
 POS_OWN, POS_RIGHT, POS_LEFT, POS_FAR = range(4)
 COLS = 256
@@ -42,7 +43,7 @@
                hid, gain, rw, ids, wg, wu, wd, sg, su, sd, x_all, gt_send, gt_all, p_all, acat,
                xg, hbuf, ybuf, sbuf, d2d, tbuf, hop, rel, froml, fromr, hsh, shared,
                in_sem, w_sem,
-               ring_s, cross_s, tile_s, d2d_s, hop_s, dir_s, rel_s, ag_r, cross_r, tile_r, d2d_r, hop_r, end_r):
+               ring_s, cross_s, tile_s, d2d_s, ret_s, ag_r, cross_r, tile_r, d2d_r, hop_r, end_r):
     chips = ep_size // CORES
     tok, dim = hid.shape
     n_exp, _, inter = wg.shape
@@ -85,7 +86,7 @@
     fetches += [(wd_h.at[:, :, early], wd.at[:, :, early]), (wd_h.at[:, :, late], wd.at[:, :, late]), (sg_h, sg), (su_h, su), (sd_h, sd)]
     weights = []
     for i, (s, d) in enumerate(fetches):
-        weights.append(pltpu.make_async_copy(s, d, w_sem.at[i]))
+        weights.append(pltpu.make_async_copy(s, d, w_sem.at[min(i, 6)]))
         weights[-1].start(priority=1)
 
     barrier = pltpu.get_barrier_semaphore()
@@ -116,9 +117,15 @@
         remote(src, dst, dev(chip, other), cross_s, r_sem)
 
     ra, lb = [], []
-    for k in range(2):
+
+    def own_rows(k):
         ra.append(spread(chip, side_a[k], right, ag_r.at[k]))
         lb.append(spread(chip, side_b[k], left, ag_r.at[2 + k]))
+        spread(chip, side_b[k], right, ag_r.at[4 + k])
+        spread(chip, side_a[k], left, ag_r.at[4 + k])
+
+    own_rows(0)
+    cross(chip, slice(0, dim), cross_r.at[0])
 
     with jax.named_scope("router"):
         ins[2].wait()
@@ -140,19 +147,18 @@
             to = (me + k) % ep_size
             remote(gt_send.at[to], gt_all.at[slot(chip, core, to // CORES, to % CORES)], {"ep": to}, tile_s, tile_r)
 
-    for k in range(2):
-        spread(chip, side_b[k], right, ag_r.at[4 + k])
-        spread(chip, side_a[k], left, ag_r.at[4 + k])
-    cross(chip, slice(0, dim), cross_r.at[0])
-
-    with jax.named_scope("relays"):
-        for k in range(2):
+    own_rows(1)
+
+    def pass_on(k):
+        with jax.named_scope(f"relays{k}"):
             ra[k].wait_recv()
-            spread(left, side_a[k], right, ag_r.at[6 + 2 * k], HUB)
+            spread(left, side_a[k], right, ag_r.at[6 + k], HUB)
             cross(left, side_a[k], cross_r.at[1 + k])
             lb[k].wait_recv()
-            spread(right, side_b[k], left, ag_r.at[7 + 2 * k], HUB)
+            spread(right, side_b[k], left, ag_r.at[6 + k], HUB)
             cross(right, side_b[k], cross_r.at[1 + k])
+
+    pass_on(0)
 
     def near_rest(k):
         with jax.named_scope(f"rest{k}"):
@@ -209,20 +215,19 @@
         with jax.named_scope(f"far{k}"):
             @pl.when(core == HUB)
             def _():
-                for r_sem, cols in ((6 + 2 * k, side_a[k]), (7 + 2 * k, side_b[k])):
-                    await_all(x_all.at[far_slots, :, cols], ag_r.at[r_sem])
+                await_all(x_all.at[far_slots, :, chunk[k]], ag_r.at[6 + k])
                 for i in range(CORES):
                     src, dst = x_all.at[ep_size - 1 - i, :, chunk[k]], x_all.at[ep_size - CORES + i, :, chunk[k]]
                     remote(src, dst, dev(chip, other), cross_s, cross_r.at[3 + k])
 
-    def gate_up(k):
+    def gate_up(k, first, end):
         def gather_far(p):
             two = slice(2 * p * cap, 2 * (p + 1) * cap)
             xg[two, chunk[k]] = xg[two, chunk[k]] + dot(p_all[two, n_near:], x_rest[:, :, chunk[k]].reshape(rows - n_near, -1)).astype(BF16)
 
-        gather_far(0)
-        for e in range(n_exp):
-            if e % 2 == 0 and e + 2 < n_exp:
+        gather_far(first // 2)
+        for e in range(first, end):
+            if e % 2 == 0 and e + 2 < end:
                 gather_far(e // 2 + 1)
             own = slice(e * cap, (e + 1) * cap)
             row = e % 4 * cap
@@ -241,19 +246,22 @@
                 for c in range(2):
                     hbuf[own, c * COLS : (c + 1) * COLS] = (jax.nn.silu(h[c]) * h[2 + c]).astype(BF16)
 
+    pass_on(1)
     near_rest(0)
     gather_near(0)
     near_rest(1)
     pass_far(0)
     gather_near(1)
-    pass_far(1)
     with jax.named_scope("farwait0"):
         await_all(x_all.at[0 : chips - 2, :, chunk[0]], cross_r.at[1])
         far_wait(0)
         weights[0].wait()
         weights[1].wait()
     with jax.named_scope("gateup0"):
-        gate_up(0)
+        gate_up(0, 0, SPLIT)
+    pass_far(1)
+    with jax.named_scope("gateup0b"):
+        gate_up(0, SPLIT, n_exp)
     with jax.named_scope("farwait1"):
         await_all(x_all.at[0 : chips - 2, :, chunk[1]], cross_r.at[2])
         far_wait(1)
@@ -279,30 +287,29 @@
         part.append(remote(sbuf.at[j, 1], d2d.at[j], dev(chip, other), d2d_s, d2d_r.at[j]))
 
     lo, up = slice(0, hc), slice(hc, COLS)
-    half_blk = n_blk // 2
+    late_blk = n_blk - 1
 
     def send(j):
         part[j].wait_recv()
         tbuf[j] = (sbuf[j, 0] + d2d[j]).reshape(chips, tok, COLS)
-        remote(tbuf.at[j, POS_FAR, :, lo], hop.at[j, :, lo], dev(right, core), hop_s, hop_r.at[j])
-        remote(tbuf.at[j, POS_FAR, :, up], hop.at[j, :, up], dev(left, core), hop_s, hop_r.at[j])
+        remote(tbuf.at[j, POS_FAR, :, lo], hop.at[j, :, lo], dev(right, core), ret_s, hop_r.at[j])
+        remote(tbuf.at[j, POS_FAR, :, up], hop.at[j, :, up], dev(left, core), ret_s, hop_r.at[j])
 
     def direct(j):
-        remote(tbuf.at[j, POS_RIGHT, :, up], froml.at[j, :, up], dev(right, core), dir_s, end_r.at[0, j // half_blk])
-        remote(tbuf.at[j, POS_LEFT, :, lo], fromr.at[j, :, lo], dev(left, core), dir_s, end_r.at[1, j // half_blk])
+        remote(tbuf.at[j, POS_RIGHT, :, up], froml.at[j, :, up], dev(right, core), ret_s, end_r.at[j // late_blk])
+        remote(tbuf.at[j, POS_LEFT, :, lo], fromr.at[j, :, lo], dev(left, core), ret_s, end_r.at[j // late_blk])
 
     def relay(j):
         await_all(hop.at[j], hop_r.at[j])
         rel[j, :, lo] = hop[j, :, lo] + tbuf[j, POS_RIGHT, :, lo]
         rel[j, :, up] = hop[j, :, up] + tbuf[j, POS_LEFT, :, up]
-        remote(rel.at[j, :, lo], froml.at[j, :, lo], dev(right, core), rel_s, end_r.at[0, j // half_blk])
-        remote(rel.at[j, :, up], fromr.at[j, :, up], dev(left, core), rel_s, end_r.at[1, j // half_blk])
+        remote(rel.at[j, :, lo], froml.at[j, :, lo], dev(right, core), ret_s, end_r.at[j // late_blk])
+        remote(rel.at[j, :, up], fromr.at[j, :, up], dev(left, core), ret_s, end_r.at[j // late_blk])
 
     def finish(k):
-        blks = slice(k * half_blk, (k + 1) * half_blk)
-        await_all(froml.at[blks], end_r.at[0, k])
-        await_all(fromr.at[blks], end_r.at[1, k])
-        for j in range(k * half_blk, (k + 1) * half_blk):
+        blks = range(late_blk) if k == 0 else range(late_blk, n_blk)
+        await_all(tbuf.at[blks[0] : blks[-1] + 1, 0:2], end_r.at[k])
+        for j in blks:
             cols = slice(j * COLS, (j + 1) * COLS)
             routed = (tbuf[j, POS_OWN] + froml[j]) + fromr[j]
             out_ref[:, cols] = ((hid[:, cols].astype(F32) + shared[:, cols].astype(F32)) + routed).astype(BF16)
@@ -312,7 +319,7 @@
             f(j)
 
     with jax.named_scope("gateup1"):
-        gate_up(1)
+        gate_up(1, 0, n_exp)
         last(0)
         compute(0)
     weights[5].wait()
@@ -325,8 +332,7 @@
     scoped(send, n_blk - 1)
 
     with jax.named_scope("shared"):
-        for copy in weights[6:]:
-            copy.wait()
+        await_all(wg.at[0 : 3 * sd.shape[0] // inter], w_sem.at[6])
         xs = x_all[0]
         mid_cols = hsh.shape[1] // 2
 
@@ -358,9 +364,7 @@
 
         await_all(gt_send.at[0 : ep_size - 1], tile_s)
         await_all(d2d, d2d_s)
-        await_all(hop, hop_s)
-        await_all(froml, dir_s)
-        await_all(rel, rel_s)
+        await_all(tbuf.at[:, 0:3], ret_s)
 
 
 def put_kernel(src, dst, o_sem):
@@ -394,8 +398,8 @@
             vm((8, CORES, chips * tok, COLS), F32), vm((n_blk, chips * tok, COLS), F32), vm((n_blk, chips, tok, COLS), F32),
             vm((n_blk, tok, COLS), F32), vm((n_blk, tok, COLS), F32), vm((n_blk, tok, COLS), F32), vm((n_blk, tok, COLS), F32),
             vm((tok, s_inter), BF16), vm((tok, dim), BF16),
-            sem((4,)), sem((9,)), sem, sem, sem, sem, sem, sem, sem,
-            sem((10,)), sem((5,)), sem, sem((n_blk,)), sem((n_blk,)), sem((2, 2)),
+            sem((4,)), sem((7,)), sem, sem, sem, sem, sem,
+            sem((8,)), sem((5,)), sem, sem((n_blk,)), sem((n_blk,)), sem((2,)),
         ]
         result = pl.pallas_call(
             functools.partial(moe_kernel, ep_size, cap),

time: 32.8 us -> 32.5 us (level)
  no operation moved by 1% of the time
where the time goes in v8:
time: 32.5 us
  Pallas kernels  31.8 us (98%)
  local copies, waits for them, and re-layouts  0.66 us (2%)
    pallas_call x1, Pallas kernels, local_block(): pl.pallas_call(functools.partial(moe_kernel, ep_size, cap), out_shape=plt...  31.8 us
    unnamed x1, local copies, waits for them, and re-layouts  0.66 us

profile of v8, /device:TPU:112, one launch (start us, length us, event | category | flops | bytes accessed | tf_op | source)
XLA Modules:
  0.0 32.5 jit_solution(17512038755002430481)
XLA Ops:
  0.0 31.8 %moe_block.1 = bf16[48,1536]{1,0:T(8,128)(2,1)S(1)} custom-call(bf16[48,1536]{1,0:T(8,128)(2,1)} %hid_h.1, f32[12,128]{1,0:T(8,128)} %bitcast.2, f32[64,1536]{1,0:T(8,128)} %rw_h.1, bf16[8,1536,512]{2,1,0:T(8,128)(2,1)} %wg_h.1, bf16[8,1536,512]{2,1,0:T(8,128)(2,1)} %wu_h.1, bf16[8,512,1536]{2,1,0:T(8,128)(2,1)} %wd_h.1, bf16[1536,1024]{1,0:T(8,128)(2,1)} %sg_h.1, ...), custom_call_target="tpu_custom_call" | custom-call | tf_op jit(solution)/shard_map/moe_block/pallas_call | solution.py:404
  31.8 0.7 %copy.12 = bf16[48,1536]{1,0:T(8,128)(2,1)} copy(bf16[48,1536]{1,0:T(8,128)(2,1)S(1)} %moe_block.1) | data formatting | bytes 294912

commit v9 on v8

--- a/solution.py
+++ b/solution.py
@@ -342,10 +342,10 @@
 
         scoped(relay, 0)
         scoped(relay, 1)
-        scoped(direct, n_blk - 1)
         shared_part(0)
         scoped(relay, 2)
         scoped(relay, 3)
+        scoped(direct, n_blk - 1)
         shared_part(1)
         scoped(relay, 4)
         scoped(relay, 5)

time: 32.5 us -> 32.5 us (level)
  no operation moved by 1% of the time
where the time goes in v9:
time: 32.5 us
  Pallas kernels  31.8 us (98%)
  local copies, waits for them, and re-layouts  0.66 us (2%)
    pallas_call x1, Pallas kernels, local_block(): pl.pallas_call(functools.partial(moe_kernel, ep_size, cap), out_shape=plt...  31.8 us
    unnamed x1, local copies, waits for them, and re-layouts  0.66 us

profile of v9, /device:TPU:112, one launch (start us, length us, event | category | flops | bytes accessed | tf_op | source)
XLA Modules:
  0.0 32.5 jit_solution(14672871199717082546)
XLA Ops:
  0.0 31.8 %moe_block.1 = bf16[48,1536]{1,0:T(8,128)(2,1)S(1)} custom-call(bf16[48,1536]{1,0:T(8,128)(2,1)} %hid_h.1, f32[12,128]{1,0:T(8,128)} %bitcast.2, f32[64,1536]{1,0:T(8,128)} %rw_h.1, bf16[8,1536,512]{2,1,0:T(8,128)(2,1)} %wg_h.1, bf16[8,1536,512]{2,1,0:T(8,128)(2,1)} %wu_h.1, bf16[8,512,1536]{2,1,0:T(8,128)(2,1)} %wd_h.1, bf16[1536,1024]{1,0:T(8,128)(2,1)} %sg_h.1, ...), custom_call_target="tpu_custom_call" | custom-call | tf_op jit(solution)/shard_map/moe_block/pallas_call | solution.py:404
  31.8 0.7 %copy.12 = bf16[48,1536]{1,0:T(8,128)(2,1)} copy(bf16[48,1536]{1,0:T(8,128)(2,1)S(1)} %moe_block.1) | data formatting | bytes 294912

commit v10 on v9

--- a/solution.py
+++ b/solution.py
@@ -130,8 +130,9 @@
     with jax.named_scope("router"):
         ins[2].wait()
         ins[3].wait()
-        r_hi, r_mid, r_low = split3(rw[...])
-        logits = (dot_t(r_low, x_norm) + dot_t(r_mid, x_norm)) + dot_t(r_hi, x_norm)
+        n_all = rw.shape[0]
+        terms = dot_t(jnp.concatenate(split3(rw[...]), axis=0), x_norm)
+        logits = (terms[2 * n_all :, :] + terms[n_all : 2 * n_all, :]) + terms[:n_all, :]
         scores = 1.0 / (1.0 + jnp.exp(-logits))
         exp_no = lax.broadcasted_iota(jnp.int32, logits.shape, 0)
         chosen = exp_no == ids[0:1, :]

time: 32.5 us -> 32.5 us (level)
  no operation moved by 1% of the time
where the time goes in v10:
time: 32.5 us
  Pallas kernels  31.8 us (98%)
  local copies, waits for them, and re-layouts  0.66 us (2%)
    pallas_call x1, Pallas kernels, local_block(): pl.pallas_call(functools.partial(moe_kernel, ep_size, cap), out_shape=plt...  31.8 us
    unnamed x1, local copies, waits for them, and re-layouts  0.66 us

profile of v10, /device:TPU:112, one launch (start us, length us, event | category | flops | bytes accessed | tf_op | source)
XLA Modules:
  0.0 32.5 jit_solution(14834233664448632179)
XLA Ops:
  0.0 31.8 %moe_block.1 = bf16[48,1536]{1,0:T(8,128)(2,1)S(1)} custom-call(bf16[48,1536]{1,0:T(8,128)(2,1)} %hid_h.1, f32[12,128]{1,0:T(8,128)} %bitcast.2, f32[64,1536]{1,0:T(8,128)} %rw_h.1, bf16[8,1536,512]{2,1,0:T(8,128)(2,1)} %wg_h.1, bf16[8,1536,512]{2,1,0:T(8,128)(2,1)} %wu_h.1, bf16[8,512,1536]{2,1,0:T(8,128)(2,1)} %wd_h.1, bf16[1536,1024]{1,0:T(8,128)(2,1)} %sg_h.1, ...), custom_call_target="tpu_custom_call" | custom-call | tf_op jit(solution)/shard_map/moe_block/pallas_call | solution.py:405
  31.8 0.7 %copy.12 = bf16[48,1536]{1,0:T(8,128)(2,1)} copy(bf16[48,1536]{1,0:T(8,128)(2,1)S(1)} %moe_block.1) | data formatting | bytes 294912
